TPU v7x, 32 devices: a whole 2x2x4 slice. The times are simulated.
32 devices in a mesh: ent: 16 (over z, y, x), dim: 2 (over core).
Axes of the slice: x: 2, y: 2, z: 4, core: 2. Of those that a mesh axis runs over, the one named last changes fastest.
Arguments:
- entities: float32 [32768, 1024], P('ent', 'dim'), may hold values from -3 to 3
- ent_state: float32 [32768], P('ent'), may hold values from 0.01 to 0.1
- buckets: int32 [32768], P('ent'), may hold values from 0 to 7
- relations: float32 [4096, 1024], P(None, 'dim'), may hold values from -1.6 to 1.6
- rel_state: float32 [4096], replicated, may hold values from 0.05 to 0.5
- triples: int32 [3, 8192], P(None, 'ent'), may hold values from 0 to 32767, as said below
- negatives: int32 [32, 256], P('ent'), may hold values from 0 to 32767, as said below
Outputs:
- new_entities: float32 [32768, 1024], P('ent', 'dim')
- new_relations: float32 [4096, 1024], P(None, 'dim')
Inputs may be any that keep to these rules, and one draw needn't show every extreme that they name: `triples`: rows 0 and 2 hold entity ids, row 1 relation ids below 4096. The block of an entity id is id // 2048. Among the 768 ids of one group (its heads, its tails and its negatives) at most 128 lie in one block, and in every draw, for each rank of a group among the 2 groups of an index of ent, some block holds exactly 128 ids of that group on every index of ent. `negatives`: entity ids; they count in the bound on the ids of a group stated for triples.
All inputs are finite; a program needn't handle non-finite values.
Results may differ from a plain program's by a relative error of at most 0.0017.
Values may be sent and summed in bfloat16 or wider, within the bound.
A program may use at most 128 MiB of HBM per device.

v0:
```python
import jax
import jax.numpy as jnp
from jax import lax
from jax.sharding import PartitionSpec as P

RANK = 512
BLK = 64


LEARN_RATE = 0.1
REG_WEIGHT = 0.01


def halves(values):
    shaped = values.reshape(values.shape[:-1] + (values.shape[-1] // (2 * BLK), 2, BLK))
    return (shaped[..., 0, :], shaped[..., 1, :])


def joined(real_part, imag_part):
    stacked = jnp.stack([real_part, imag_part], axis=-2)
    return stacked.reshape(stacked.shape[:-3] + (stacked.shape[-3] * 2 * BLK,))


def complex_product(former, latter):
    former_re, former_im = halves(former)
    latter_re, latter_im = halves(latter)
    return joined(
        former_re * latter_re - former_im * latter_im, former_re * latter_im + former_im * latter_re
    )


def conjugate(values):
    real_part, imag_part = halves(values)
    return joined(real_part, -imag_part)


def rounded(values):
    return lax.optimization_barrier(values.astype(jnp.bfloat16))


def contract_first(former, latter):
    return lax.dot_general(
        former, latter, (((0,), (0,)), ((), ())), preferred_element_type=jnp.float32
    )


def contract_last(former, latter):
    return lax.dot_general(
        former, latter, (((1,), (1,)), ((), ())), preferred_element_type=jnp.float32
    )


def exchange(blocks):
    return [
        lax.all_to_all(block, "ent", split_axis=0, concat_axis=0, tiled=True) for block in blocks
    ]


def group_step(rows_group, rel_float, group_len):
    head_float = rows_group[:group_len].astype(jnp.float32)
    tail_float = rows_group[group_len : 2 * group_len].astype(jnp.float32)
    noise_rows = rows_group[2 * group_len :]
    width_neg = noise_rows.shape[0]
    query = rounded(complex_product(head_float, rel_float))
    probe = rounded(complex_product(conjugate(rel_float), tail_float))
    part_pos = jnp.sum(query.astype(jnp.float32) * tail_float, axis=-1, keepdims=True)
    part = jnp.concatenate(
        [
            contract_last(query, noise_rows),
            contract_last(probe, noise_rows),
            jnp.broadcast_to(part_pos, (group_len, 128)),
        ],
        axis=1,
    ).astype(jnp.bfloat16)
    scores = jnp.sum(lax.all_gather(part, "dim").astype(jnp.float32), axis=0)
    both_coef = rounded(jax.nn.sigmoid(scores[:, : 2 * width_neg]) / width_neg)
    pos_float = -jax.nn.sigmoid(-scores[:, 2 * width_neg : 2 * width_neg + 1])
    pos_float = rounded(pos_float).astype(jnp.float32)
    tail_coef = both_coef[:, :width_neg]
    head_coef = both_coef[:, width_neg:]
    tail_pull = pos_float * tail_float + jnp.dot(
        tail_coef, noise_rows, preferred_element_type=jnp.float32
    )
    head_pull = jnp.dot(head_coef, noise_rows, preferred_element_type=jnp.float32)
    head_side = pos_float * head_float + head_pull
    head_grad = complex_product(conjugate(rel_float), tail_pull).astype(jnp.bfloat16)
    tail_grad = complex_product(rel_float, head_side).astype(jnp.bfloat16)
    noise_grad = (contract_first(tail_coef, query) + contract_first(head_coef, probe)).astype(
        jnp.bfloat16
    )
    rel_grad = complex_product(conjugate(head_float), tail_pull) + complex_product(
        tail_float, conjugate(head_pull)
    )
    return (
        jnp.concatenate([head_grad, tail_grad, noise_grad], axis=0),
        rel_grad.astype(jnp.bfloat16),
    )


def placement_of(wanted_row, owners, rows_here, slot_count):
    request_count = wanted_row.shape[0]
    owner_of = wanted_row // rows_here
    owner_hits = (owner_of[:, None] == jnp.arange(owners, dtype=jnp.int32)[None, :]).astype(
        jnp.bfloat16
    )
    order = jnp.arange(request_count, dtype=jnp.int32)
    earlier = (order[:, None] > order[None, :]).astype(jnp.bfloat16)
    before = jnp.dot(earlier, owner_hits, preferred_element_type=jnp.float32)
    slot_rank = jnp.sum(before * owner_hits.astype(jnp.float32), axis=-1).astype(jnp.int32)
    slot_flat = owner_of * slot_count + slot_rank
    matches = slot_flat[:, None] == jnp.arange(owners * slot_count, dtype=jnp.int32)[None, :]
    slot_ids = jnp.sum(jnp.where(matches, wanted_row[:, None] + 1, 0), axis=0) - 1
    return (matches.astype(jnp.bfloat16), slot_ids.reshape(owners, slot_count))


def accumulate(local_rows, received_rows, totals, counts):
    flat_rows = received_rows.reshape(local_rows.shape[0], received_rows.shape[-1])
    positions = jnp.arange(totals.shape[0], dtype=jnp.int32)
    one_hot = (local_rows[:, None] == positions[None, :]).astype(jnp.bfloat16)
    totals = totals + contract_first(one_hot, flat_rows)
    counts = counts + jnp.sum(one_hot, axis=0, dtype=jnp.float32)
    return (totals, counts)


def teams(owners):
    near_size = 4 if owners % 4 == 0 else 1
    far_size = owners // near_size
    near = [[row * near_size + place for place in range(near_size)] for row in range(far_size)]
    far = [[row * near_size + place for row in range(far_size)] for place in range(near_size)]
    return (near, far)


def sum_relations(rel_rows, near_ids, rel_count, near, far):
    near_size, far_size = len(far), len(near)
    row_count, columns = rel_rows.shape
    tiles = rel_rows.reshape(row_count, near_size, columns // near_size).transpose(1, 0, 2)
    tiles = lax.all_to_all(
        tiles, "ent", split_axis=0, concat_axis=0, axis_index_groups=near, tiled=True
    )
    hits = (near_ids[:, None] == jnp.arange(rel_count, dtype=jnp.int32)[None, :]).astype(
        jnp.bfloat16
    )
    part = contract_first(hits, tiles.reshape(near_size * row_count, columns // near_size)).astype(
        jnp.bfloat16
    )
    share = lax.psum_scatter(
        part, "ent", scatter_dimension=0, axis_index_groups=far, tiled=True
    )
    whole = lax.all_gather(share, "ent", axis=0)
    whole = whole.reshape(far_size, near_size, rel_count // far_size, columns // near_size)
    return whole.transpose(0, 2, 1, 3).reshape(rel_count, columns).astype(jnp.float32)


def adagrad(table, state, grad, squares):
    new_state = state + squares / (2 * RANK)
    scale = LEARN_RATE / jnp.sqrt(new_state)
    return table - grad * scale[:, None]


def per_device(entities, ent_state, buckets, relations, rel_state, triples, negatives):
    owners = lax.axis_size("ent")
    rows_here, columns_here = entities.shape
    rel_count = relations.shape[0]
    row_base = lax.axis_index("ent") * rows_here
    groups_here = negatives.shape[0]
    group_len = triples.shape[1] // groups_here
    request_count = 2 * group_len + negatives.shape[1]
    slot_count = 8 * ((request_count + 3 * owners - 1) // (3 * owners))
    ent_low = entities.astype(jnp.bfloat16)
    head_ids = triples[0].reshape(groups_here, group_len)
    tail_ids = triples[2].reshape(groups_here, group_len)
    wanted = jnp.concatenate([head_ids, tail_ids, negatives], axis=1)
    placed = [
        placement_of(wanted[index], owners, rows_here, slot_count) for index in range(groups_here)
    ]
    near, far = teams(owners)
    near_ids = lax.all_gather(triples[1], "ent", axis_index_groups=near, tiled=True)
    slot_ids = jnp.stack([slots for _, slots in placed], axis=1)
    received = lax.all_to_all(slot_ids, "ent", split_axis=0, concat_axis=0, tiled=True)
    local_rows = [received[:, index].reshape(-1) - row_base for index in range(groups_here)]
    looked_up = [
        jnp.take(ent_low, rows, axis=0, mode="clip").reshape(
            owners, slot_count, columns_here
        )
        for rows in local_rows
    ]
    arrived = exchange(looked_up)
    rel_float = rounded(jnp.take(relations, triples[1], axis=0, mode="clip")).astype(jnp.float32)
    outgoing, rel_rows = [], []
    for index in range(groups_here):
        matches = placed[index][0]
        rows_group = jnp.dot(
            matches,
            arrived[index].reshape(owners * slot_count, columns_here),
            preferred_element_type=jnp.float32,
        ).astype(jnp.bfloat16)
        grads, rel_row = group_step(
            rows_group, rel_float[index * group_len : (index + 1) * group_len], group_len
        )
        sent = (
            contract_first(matches, grads)
            .astype(jnp.bfloat16)
            .reshape(owners, slot_count, columns_here)
        )
        if index + 1 < groups_here:
            sent, arrived[index + 1] = lax.optimization_barrier((sent, arrived[index + 1]))
        outgoing.append(sent)
        rel_rows.append(rel_row)
    rel_grad = sum_relations(jnp.concatenate(rel_rows, axis=0), near_ids, rel_count, near, far)
    returned = exchange(outgoing)
    totals = jnp.zeros((rows_here, columns_here), jnp.float32)
    counts = jnp.zeros((rows_here,), jnp.float32)
    for index in range(groups_here):
        totals, counts = accumulate(local_rows[index], returned[index], totals, counts)
    weight = REG_WEIGHT * (buckets.astype(jnp.float32) + 1.0) * counts
    totals = totals + weight[:, None] * 3.0 * entities * jnp.abs(entities)
    ent_squares = jnp.sum(totals * totals, axis=-1)
    ent_all, rel_all = lax.psum((ent_squares, jnp.sum(rel_grad * rel_grad, axis=-1)), "dim")
    new_relations = adagrad(relations, rel_state, rel_grad, rel_all)
    new_entities = adagrad(entities, ent_state, totals, ent_all)
    return (new_entities, new_relations)


def solution(mesh):
    placed = (
        P("ent", "dim"),
        P("ent"),
        P("ent"),
        P(None, "dim"),
        P(),
        P(None, "ent"),
        P("ent", None),
    )
    return jax.shard_map(
        per_device,
        mesh=mesh,
        in_specs=placed,
        out_specs=(P("ent", "dim"), P(None, "dim")),
        check_vma=False,
    )
```

profile of v0, /device:TPU:13, one launch (start us, length us, event | category | flops | bytes accessed | tf_op | source)
XLA Modules:
  0.0 409.4 jit_solution(17636354440529703122)
XLA Ops:
  11.9 6.6 %all-to-all-start = ((s32[16,2,128]{2,1,0:T(2,128)}), s32[16,2,128]{2,1,0:T(2,128)S(1)}, u32[]{:S(2)}, u32[]{:S(2)}) async-start(s32[16,2,128]{2,1,0:T(2,128)} %pad_add_fusion), calls=%async_computation | async-start | bytes 32768 | tf_op jit(solution)/shard_map/all_to_all | solution.py:179
  22.8 9.2 %gather_fusion.1 = bf16[2048,512]{1,0:T(8,128)(2,1)} fusion(bf16[2048,512]{1,0:T(8,128)(2,1)S(1)} %convert_element_type.201, s32[2048]{0:T(1024)S(1)} %broadcast_clamp_fusion.1), kind=kCustom, calls=%fused_computation.1 | custom fusion | bytes 4202496 | tf_op jit(solution)/shard_map/jit(_take)/gather | solution.py:182
  32.0 6.2 %all-to-all-start.1 = ((bf16[16,128,512]{2,1,0:T(8,128)(2,1)}), bf16[16,128,512]{2,1,0:T(8,128)(2,1)}, u32[]{:S(2)}, u32[]{:S(2)}) async-start(bf16[16,128,512]{2,1,0:T(8,128)(2,1)} %bitcast.78), calls=%async_computation.1 | async-start | bytes 4194304 | tf_op jit(solution)/shard_map/all_to_all | solution.py:55
  38.3 5.4 %gather_fusion = bf16[512,512]{1,0:T(8,128)(2,1)S(1)} fusion(f32[4096,512]{1,0:T(8,128)} %param.10, s32[1024]{0:T(1024)S(1)} %pad_clamp_fusion), kind=kCustom, calls=%fused_computation | custom fusion | bytes 1050624 | tf_op jit(solution)/shard_map/jit(_take)/gather | solution.py:188
  46.0 7.1 %all-gather = s32[1,2048]{1,0:T(1,128)} all-gather(s32[1,512]{1,0:T(1,128)S(1)} %get-tuple-element.66), channel_id=2, replica_groups={{0,2,4,6},{8,10,12,14},{16,18,20,22},{24,26,28,30},{1,3,5,7},{9,11,13,1..., dimensions={1}, use_global_device_ids=true | all-gather | bytes 10240 | tf_op jit(solution)/shard_map/all_gather | solution.py:177
  53.1 9.2 %gather_fusion.2 = bf16[2048,512]{1,0:T(8,128)(2,1)} fusion(bf16[2048,512]{1,0:T(8,128)(2,1)S(1)} %convert_element_type.201, s32[2048]{0:T(1024)S(1)} %broadcast_clamp_fusion), kind=kCustom, calls=%fused_computation.2 | custom fusion | bytes 4202496 | tf_op jit(solution)/shard_map/jit(_take)/gather | solution.py:182
  62.4 24.3 %all-to-all-done.1 = bf16[16,128,512]{2,1,0:T(8,128)(2,1)} async-done(((bf16[16,128,512]{2,1,0:T(8,128)(2,1)}), bf16[16,128,512]{2,1,0:T(8,128)(2,1)}, u32[]{:S(2)}, u32[]{:S(2)}) %all-to-all-start.1) | async-done | bytes 2097184 | tf_op jit(solution)/shard_map/all_to_all | solution.py:55
  112.5 26.7 %all-to-all-done.2 = bf16[16,128,512]{2,1,0:T(8,128)(2,1)} async-done(((bf16[16,128,512]{2,1,0:T(8,128)(2,1)}), bf16[16,128,512]{2,1,0:T(8,128)(2,1)}, u32[]{:S(2)}, u32[]{:S(2)}) %all-to-all-start.2) | async-done | bytes 2097184 | tf_op jit(solution)/shard_map/all_to_all | solution.py:55
  165.2 5.9 %all-to-all-done.5 = bf16[4,512,128]{2,1,0:T(8,128)(2,1)S(1)} async-done(((bf16[4,512,128]{2,1,0:T(8,128)(2,1)}), bf16[4,512,128]{2,1,0:T(8,128)(2,1)S(1)}, u32[]{:S(2)}, u32[]{:S(2)}) %all-to-all-start.5) | async-done | bytes 524320 | tf_op jit(solution)/shard_map/all_to_all | solution.py:137
  171.2 10.2 %fusion.13 = bf16[4096,128]{1,0:T(8,128)(2,1)} fusion(bf16[2048,128]{1,0:T(8,128)(2,1)S(1)} %bitcast.117, s32[2048]{0:T(1024)S(1)} %bitcast.133), kind=kOutput, calls=%fused_computation.27 | convolution fusion | flops 2156396544 | bytes 1581056 | tf_op jit(solution)/shard_map/dot_general | solution.py:42
  184.7 4.9 %all-to-all-start.4 = ((bf16[16,128,512]{2,1,0:T(8,128)(2,1)}), bf16[16,128,512]{2,1,0:T(8,128)(2,1)S(1)}, u32[]{:S(2)}, u32[]{:S(2)}) async-start(bf16[16,128,512]{2,1,0:T(8,128)(2,1)} %bitcast.106), calls=%async_computation.4 | async-start | bytes 4194304 | tf_op jit(solution)/shard_map/all_to_all | solution.py:55
  189.7 33.0 %reduce-scatter.2.cloned.1.call-done = bf16[1024,128]{1,0:T(8,128)(2,1)} async-done(((bf16[4096,128]{1,0:T(8,128)(2,1)}), bf16[1024,128]{1,0:T(8,128)(2,1)}) %reduce-scatter.2.cloned.1.call-update) | async-done | bytes 262160 | tf_op jit(solution)/shard_map/reduce_scatter | solution.py:146
  222.7 33.2 %all-to-all-done.4 = bf16[16,128,512]{2,1,0:T(8,128)(2,1)S(1)} async-done(((bf16[16,128,512]{2,1,0:T(8,128)(2,1)}), bf16[16,128,512]{2,1,0:T(8,128)(2,1)S(1)}, u32[]{:S(2)}, u32[]{:S(2)}) %all-to-all-start.4) | async-done | bytes 2097184 | tf_op jit(solution)/shard_map/all_to_all | solution.py:55
  255.9 4.6 %all-to-all-start.3 = ((bf16[16,128,512]{2,1,0:T(8,128)(2,1)}), bf16[16,128,512]{2,1,0:T(8,128)(2,1)}, u32[]{:S(2)}, u32[]{:S(2)}) async-start(bf16[16,128,512]{2,1,0:T(8,128)(2,1)} %bitcast.18), calls=%async_computation.3 | async-start | bytes 4194304 | tf_op jit(solution)/shard_map/all_to_all | solution.py:55
  260.5 5.7 %copy.141 = f32[2048,512]{0,1:T(8,128)} copy(f32[2048,512]{1,0:T(8,128)} %param.7) | data formatting | bytes 8388608 | tf_op args[0]
  270.4 7.2 %fusion.3 = f32[2048,512]{0,1:T(8,128)} fusion(bf16[2048,512]{1,0:T(8,128)(2,1)S(1)} %bitcast.105, s32[2048]{0:T(1024)S(1)} %bitcast.125), kind=kOutput, calls=%fused_computation.10 | convolution fusion | flops 4299161600 | bytes 6299648 | tf_op jit(solution)/shard_map/dot_general | solution.py:42
  277.6 64.2 %all-to-all-done.3 = bf16[16,128,512]{2,1,0:T(8,128)(2,1)} async-done(((bf16[16,128,512]{2,1,0:T(8,128)(2,1)}), bf16[16,128,512]{2,1,0:T(8,128)(2,1)}, u32[]{:S(2)}, u32[]{:S(2)}) %all-to-all-start.3) | async-done | bytes 2097184 | tf_op jit(solution)/shard_map/all_to_all | solution.py:55
  341.8 12.2 %multiply_reduce_fusion.1 = (f32[2048]{0:T(1024)S(1)}, f32[2048,512]{0,1:T(8,128)}) fusion(f32[2048,512]{0,1:T(8,128)} %copy.141, f32[2048]{0:T(1024)S(1)} %multiply_multiply_fusion, f32[2048,512]{0,1:T(8,128)} %fusion.3, bf16[2048,512]{1,0:T(8,128)(2,1)} %bitcast.21, s32[2048]{0:T(1024)S(1)} %bitcast.122), kind=kOutput, calls=%fused_computation.29 | convolution fusion | flops 4306499584 | bytes 14704640 | tf_op jit(solution)/shard_map/dot_general | solution.py:42
  358.0 5.5 %all-reduce = (f32[2048]{0:T(1024)S(1)}, f32[4096]{0:T(1024)S(1)}) all-reduce(f32[2048]{0:T(1024)S(1)} %get-tuple-element.75, f32[4096]{0:T(1024)S(1)} %bitcast.119), channel_id=1, replica_groups=mesh['ent'=16,'dim'=2] {'dim'}, use_global_device_ids=true, to_apply=%region_11.12 | all-reduce | flops 6144 | bytes 49152 | tf_op jit(solution)/shard_map/psum | solution.py:218
  363.5 6.7 %multiply_subtract_fusion = f32[2048,512]{0,1:T(8,128)} fusion(f32[2048,512]{0,1:T(8,128)} %copy.141, f32[2048,512]{0,1:T(8,128)} %get-tuple-element.76, f32[2048]{0:T(1024)S(1)} %rsqrt_multiply_fusion.1), kind=kLoop, calls=%fused_computation.28 | loop fusion | flops 2097152 | bytes 12591104 | tf_op jit(solution)/shard_map/sub | solution.py:157
  370.2 5.3 %copy.147 = f32[2048,512]{1,0:T(8,128)} copy(f32[2048,512]{0,1:T(8,128)} %multiply_subtract_fusion) | data formatting | bytes 8388608
  375.5 5.3 %convert_element_type.247 = f32[16384,128]{1,0:T(8,128)} convert(bf16[16384,128]{1,0:T(8,128)(2,1)} %all-gather.4.cloned.1.call-done) | non-fusion elementwise | flops 2097152 | bytes 12582912 | tf_op jit(solution)/shard_map/convert_element_type | solution.py:151
  380.8 12.0 %copy.146 = f32[4,1024,4,128]{3,2,1,0:T(4,128)} copy(f32[4,1024,4,128]{3,1,2,0:T(8,128)} %bitcast.75) | data formatting | bytes 16777216 | tf_op jit(solution)/shard_map/convert_element_type | solution.py:151
  392.8 9.6 %fusion.6 = f32[4096,512]{1,0:T(8,128)} fusion(f32[4096,512]{1,0:T(8,128)} %param.10, f32[512,8,4,128]{3,2,1,0:T(4,128)} %bitcast.76, f32[4096]{0:T(1024)S(1)} %rsqrt_multiply_fusion), kind=kLoop, calls=%fused_computation.15 | loop fusion | flops 4194304 | bytes 25182208 | tf_op jit(solution)/shard_map/sub | solution.py:157
  (135 shorter events, 74.4 us)
Async XLA Ops:
  9.1 130.0 %copy-start.12 = (s32[768]{0:T(1024)}, s32[768]{0:T(1024)S(1)}, u32[]{:S(2)}) copy-start(s32[768]{0:T(1024)S(1)} %get-tuple-element.70) | copy-start | bytes 9220
  11.9 10.9 %all-to-all-start = ((s32[16,2,128]{2,1,0:T(2,128)}), s32[16,2,128]{2,1,0:T(2,128)S(1)}, u32[]{:S(2)}, u32[]{:S(2)}) async-start(s32[16,2,128]{2,1,0:T(2,128)} %pad_add_fusion), calls=%async_computation | async-start | bytes 32768 | tf_op jit(solution)/shard_map/all_to_all | solution.py:179
  32.0 54.7 %all-to-all-start.1 = ((bf16[16,128,512]{2,1,0:T(8,128)(2,1)}), bf16[16,128,512]{2,1,0:T(8,128)(2,1)}, u32[]{:S(2)}, u32[]{:S(2)}) async-start(bf16[16,128,512]{2,1,0:T(8,128)(2,1)} %bitcast.78), calls=%async_computation.1 | async-start | bytes 4194304 | tf_op jit(solution)/shard_map/all_to_all | solution.py:55
  86.7 52.5 %all-to-all-start.2 = ((bf16[16,128,512]{2,1,0:T(8,128)(2,1)}), bf16[16,128,512]{2,1,0:T(8,128)(2,1)}, u32[]{:S(2)}, u32[]{:S(2)}) async-start(bf16[16,128,512]{2,1,0:T(8,128)(2,1)} %bitcast.77), calls=%async_computation.2 | async-start | bytes 4194304 | tf_op jit(solution)/shard_map/all_to_all | solution.py:55
  95.0 0.7 copy-start.3
  101.4 0.8 copy-start
  107.5 1.4 copy-start.4
  107.5 1.7 copy-start.7
  143.6 6.5 %copy-start.1 = (bf16[256,4,2,64]{0,3,2,1:T(8,128)(2,1)}, bf16[256,4,2,64]{0,3,2,1:T(8,128)(2,1)S(1)}, u32[]{:S(2)}) copy-start(bf16[256,4,2,64]{0,3,2,1:T(8,128)(2,1)S(1)} %pad_maximum_fusion.7) | copy-start | bytes 786436
  153.9 4.5 %copy-start.5 = (f32[256,512]{0,1:T(8,128)S(1)}, f32[256,512]{0,1:T(8,128)}, u32[]{:S(2)}) copy-start(f32[256,512]{0,1:T(8,128)} %get-tuple-element.74) | copy-start | bytes 1572868
  158.5 6.5 %copy-start.2 = (bf16[256,4,2,64]{0,3,2,1:T(8,128)(2,1)S(1)}, bf16[256,4,2,64]{0,3,2,1:T(8,128)(2,1)}, u32[]{:S(2)}) copy-start(bf16[256,4,2,64]{0,3,2,1:T(8,128)(2,1)} %copy-done.1) | copy-start | bytes 786436
  158.5 12.7 %copy-start.10 = (s32[1,2048]{1,0:T(1,128)S(1)}, s32[1,2048]{1,0:T(1,128)}, u32[]{:S(2)}) copy-start(s32[1,2048]{1,0:T(1,128)} %all-gather) | copy-start | bytes 24580
  160.8 10.3 %all-to-all-start.5 = ((bf16[4,512,128]{2,1,0:T(8,128)(2,1)}), bf16[4,512,128]{2,1,0:T(8,128)(2,1)S(1)}, u32[]{:S(2)}, u32[]{:S(2)}) async-start(bf16[4,512,128]{2,1,0:T(8,128)(2,1)} %maximum_bitcast_fusion), calls=%async_computation.5 | async-start | bytes 1048576 | tf_op jit(solution)/shard_map/all_to_all | solution.py:137
  164.3 58.4 %reduce-scatter.2.cloned.1.call-start = ((), (), s32[]{:S(2)}) async-start(), calls=%async_computation.7 | async-start | bytes 1310720 | tf_op jit(solution)/shard_map/reduce_scatter | solution.py:146
  171.1 10.2 %copy-start.6 = (bf16[256,512]{1,0:T(8,128)(2,1)S(1)}, bf16[256,512]{1,0:T(8,128)(2,1)}, u32[]{:S(2)}) copy-start(bf16[256,512]{1,0:T(8,128)(2,1)} %copy.138) | copy-start | bytes 786436
  171.1 10.2 %copy-start.13 = (s32[768]{0:T(1024)S(1)}, s32[768]{0:T(1024)}, u32[]{:S(2)}) copy-start(s32[768]{0:T(1024)} %copy-done.12) | copy-start | bytes 9220
  184.7 71.2 %all-to-all-start.4 = ((bf16[16,128,512]{2,1,0:T(8,128)(2,1)}), bf16[16,128,512]{2,1,0:T(8,128)(2,1)S(1)}, u32[]{:S(2)}, u32[]{:S(2)}) async-start(bf16[16,128,512]{2,1,0:T(8,128)(2,1)} %bitcast.106), calls=%async_computation.4 | async-start | bytes 4194304 | tf_op jit(solution)/shard_map/all_to_all | solution.py:55
  189.6 164.3 %all-gather.4.cloned.1.call-start = ((), (), s32[]{:S(2)}) async-start(), calls=%async_computation.8 | async-start | bytes 4456448 | tf_op jit(solution)/shard_map/all_gather | solution.py:149
  255.9 85.8 %all-to-all-start.3 = ((bf16[16,128,512]{2,1,0:T(8,128)(2,1)}), bf16[16,128,512]{2,1,0:T(8,128)(2,1)}, u32[]{:S(2)}, u32[]{:S(2)}) async-start(bf16[16,128,512]{2,1,0:T(8,128)(2,1)} %bitcast.18), calls=%async_computation.3 | async-start | bytes 4194304 | tf_op jit(solution)/shard_map/all_to_all | solution.py:55
  260.5 9.9 %copy-start.11 = (s32[2048]{0:T(1024)S(1)}, s32[2048]{0:T(1024)}, u32[]{:S(2)}) copy-start(s32[2048]{0:T(1024)} %param.9) | copy-start | bytes 24580
  353.9 9.5 %copy-start.9 = (f32[2048]{0:T(1024)S(1)}, f32[2048]{0:T(1024)}, u32[]{:S(2)}) copy-start(f32[2048]{0:T(1024)} %param.8) | copy-start | bytes 24580
  380.8 12.0 %copy-start.8 = (f32[4096]{0:T(1024)S(1)}, f32[4096]{0:T(1024)}, u32[]{:S(2)}) copy-start(f32[4096]{0:T(1024)} %param.11) | copy-start | bytes 49156
Sparse Core Ops, SparseCore 0:
  181.5 41.1 reduce-scatter.1
  225.5 113.7 all-gather.3
where the time goes:
time: 416 us; the launch traced here: 409 us
  waiting for transfers between devices  189 us (45%)
  local copies, waits for them, and re-layouts  58.8 us (14%)
  matrix products  50.1 us (12%)
  other arithmetic  45.8 us (11%)
  starting transfers between devices  30.4 us (7%)
  blocking collectives  20.4 us (5%)
  between operations  14.8 us (4%)
    all_to_all x4, waiting for transfers between devices, exchange(): lax.all_to_all(block, 'ent', split_axis=0, concat_axis=0, tiled=True)  148 us
    dot_general x9, matrix products, contract_first(): lax.dot_general(former, latter, (((0,), (0,)), ((), ())), preferred_eleme...  37.3 us
    reduce_scatter x1, waiting for transfers between devices, sum_relations(): lax.psum_scatter(part, 'ent', scatter_dimension=0, axis_index_groups=far,...  33 us
    all_to_all x4, starting transfers between devices, exchange(): lax.all_to_all(block, 'ent', split_axis=0, concat_axis=0, tiled=True)  20.1 us
    gather x2, local copies, waits for them, and re-layouts, per_device(): jnp.take(ent_low, rows, axis=0, mode='clip')  18.4 us
    sub x2, other arithmetic, adagrad(): return table - grad * scale[:, None]  16.3 us
    unnamed x35, local copies, waits for them, and re-layouts  12.9 us
    convert_element_type x1, local copies, waits for them, and re-layouts, sum_relations(): whole.transpose(0, 2, 1, 3).reshape(rel_count, columns).astype(jnp.float32)  12 us
  transfers between devices with their start and end apart: 8, of which 7 were waited for; matrix products, arithmetic and copies ran while one was open for 17% of the time, Pallas kernels for 0%

commit v1 on v0

--- a/solution.py
+++ b/solution.py
@@ -1,6 +1,10 @@
+import functools
+
 import jax
 import jax.numpy as jnp
 from jax import lax
+from jax.experimental import pallas as pl
+from jax.experimental.pallas import tpu as pltpu
 from jax.sharding import PartitionSpec as P
 
 RANK = 512
@@ -9,6 +13,7 @@
 
 LEARN_RATE = 0.1
 REG_WEIGHT = 0.01
+MESH = pl.DeviceIdType.MESH
 
 
 def halves(values):
@@ -50,10 +55,348 @@
     )
 
 
-def exchange(blocks):
-    return [
-        lax.all_to_all(block, "ent", split_axis=0, concat_axis=0, tiled=True) for block in blocks
-    ]
+def position(near_size):
+    me = lax.axis_index("ent")
+    return lax.div(me, near_size), lax.rem(me, near_size)
+
+
+def greet(near_size, far_size):
+    far, near = position(near_size)
+    barrier = pltpu.get_barrier_semaphore()
+    for step in range(1, near_size):
+        peer = far * near_size + lax.rem(near + step, near_size)
+        pl.semaphore_signal(barrier, inc=1, device_id={"ent": peer}, device_id_type=MESH)
+    for step in range(1, far_size):
+        peer = lax.rem(far + step, far_size) * near_size + near
+        pl.semaphore_signal(barrier, inc=1, device_id={"ent": peer}, device_id_type=MESH)
+    pl.semaphore_wait(barrier, near_size + far_size - 2)
+
+
+def send(source, target, send_sem, recv_sem, peer):
+    return pltpu.make_async_remote_copy(
+        src_ref=source,
+        dst_ref=target,
+        send_sem=send_sem,
+        recv_sem=recv_sem,
+        device_id={"ent": peer},
+        device_id_type=MESH,
+    )
+
+
+def line_step(index, far_size):
+    return jnp.where(
+        index == far_size - 1, 0, 1 + lax.rem(far_size // 2 - 1 + index, far_size - 1)
+    )
+
+
+def fetch_kernel(
+    sizes, table, ids, maps, arrived, own_ids, line_maps,
+    line_ids, near_out, near_in, far_out,
+    ids_ss, ids_rs, maps_ss, maps_rs, fwd_ss, fwd_rs, near_ss, near_rs, far_ss, far_rs,
+):
+    near_size, far_size, groups, slots, merged = sizes
+    far, near = position(near_size)
+    rows_here = table.shape[0]
+    greet(near_size, far_size)
+
+    def line_peer(step):
+        there = lax.rem(far + step, far_size)
+        return there, there * near_size + near
+
+    def ids_copy(step):
+        there, peer = line_peer(step)
+        return send(ids.at[there], line_ids.at[far], ids_ss.at[step], ids_rs.at[step], peer)
+
+    def maps_copy(step):
+        there, peer = line_peer(step)
+        return send(maps.at[there], line_maps.at[far], maps_ss.at[step], maps_rs.at[step], peer)
+
+    def near_peer(step):
+        there = lax.rem(near + step, near_size)
+        return there, far * near_size + there
+
+    def fwd_copy(step):
+        there, peer = near_peer(step)
+        return send(
+            line_ids.at[:, there], own_ids.at[near], fwd_ss.at[step], fwd_rs.at[step], peer
+        )
+
+    for step in range(1, far_size):
+        ids_copy(step).start()
+    for step in range(1, far_size):
+        maps_copy(step).start()
+    line_ids[far] = ids[far]
+    line_maps[far] = maps[far]
+    for step in range(1, far_size):
+        ids_copy(step).wait()
+    for step in range(1, near_size):
+        fwd_copy(step).start()
+    own_ids[near] = line_ids[:, near]
+    for step in range(1, near_size):
+        fwd_copy(step).wait()
+    for step in range(1, far_size):
+        maps_copy(step).wait()
+
+    def near_copy(group, step, there):
+        beside, peer = near_peer(step)
+        return send(
+            near_out.at[group, step, there],
+            near_in.at[group, there, near],
+            near_ss.at[group, step, there],
+            near_rs.at[group, step, there],
+            peer,
+        )
+
+    def look_up(group, index):
+        step = lax.rem(index + 1, near_size)
+        there = lax.rem(far + line_step(lax.div(index, near_size), far_size), far_size)
+        beside = lax.rem(near + step, near_size)
+        wanted = jnp.transpose(own_ids[beside, there])[:slots, group : group + 1]
+        hits = (wanted == lax.broadcasted_iota(jnp.int32, (slots, rows_here), 1))
+        found = jnp.dot(
+            hits.astype(jnp.float32).astype(jnp.bfloat16), table[...], preferred_element_type=jnp.float32
+        ).astype(jnp.bfloat16)
+
+        @pl.when(step == 0)
+        def _():
+            near_in[group, there, near] = found
+
+        @pl.when(step != 0)
+        def _():
+            near_out[group, step, there] = found
+            near_copy(group, step, there).start()
+
+    def far_copy(group, there):
+        peer = there * near_size + near
+        return send(
+            far_out.at[group, there],
+            arrived.at[group, far],
+            far_ss.at[group, there],
+            far_rs.at[group, far],
+            peer,
+        )
+
+    def far_arrival(group, there):
+        peer = there * near_size + near
+        return send(
+            far_out.at[group, there],
+            arrived.at[group, there],
+            far_ss.at[group, there],
+            far_rs.at[group, there],
+            peer,
+        )
+
+    def merge(group, index):
+        there = lax.rem(far + line_step(index, far_size), far_size)
+        for step in range(1, near_size):
+            near_copy(group, step, there).wait_recv()
+        targets = line_maps[there][group : group + 1]
+        picks = (
+            lax.broadcasted_iota(jnp.int32, (merged, near_size * slots), 0) == targets
+        )
+        rows = near_in[group, there].reshape(near_size * slots, table.shape[1])
+        block = jnp.dot(
+            picks.astype(jnp.float32).astype(jnp.bfloat16), rows, preferred_element_type=jnp.float32
+        ).astype(jnp.bfloat16)
+
+        @pl.when(there == far)
+        def _():
+            arrived[group, far] = block
+
+        @pl.when(there != far)
+        def _():
+            far_out[group, there] = block
+            far_copy(group, there).start()
+
+    @pl.loop(0, far_size * near_size)
+    def _(index):
+        look_up(0, index)
+
+    for group in range(1, groups):
+
+        @pl.loop(0, far_size)
+        def _(index):
+            @pl.loop(0, near_size)
+            def _(part):
+                look_up(group, index * near_size + part)
+
+            merge(group - 1, index)
+
+    @pl.loop(0, far_size)
+    def _(index):
+        merge(groups - 1, index)
+
+    for group in range(groups):
+        for step in range(1, far_size):
+            there = lax.rem(far + step, far_size)
+            far_arrival(group, there).wait()
+        for step in range(1, near_size):
+
+            @pl.loop(0, far_size)
+            def _(there):
+                near_copy(group, step, there).wait_send()
+
+
+def fetch(table, ids, maps, sizes):
+    near_size, far_size, groups, slots, merged = sizes
+    columns = table.shape[1]
+    dma = pltpu.SemaphoreType.DMA
+    vmem = pl.BlockSpec(memory_space=pltpu.VMEM)
+    return pl.pallas_call(
+        functools.partial(fetch_kernel, sizes),
+        name="fetch_rows",
+        out_shape=(
+            jax.ShapeDtypeStruct((groups, far_size, merged, columns), jnp.bfloat16),
+            jax.ShapeDtypeStruct((near_size,) + ids.shape[:1] + ids.shape[2:], jnp.int32),
+            jax.ShapeDtypeStruct(maps.shape, jnp.int32),
+        ),
+        in_specs=[vmem] * 3,
+        out_specs=(vmem,) * 3,
+        scratch_shapes=[
+            pltpu.VMEM(ids.shape, jnp.int32),
+            pltpu.VMEM((groups, near_size, far_size, slots, columns), jnp.bfloat16),
+            pltpu.VMEM((groups, far_size, near_size, slots, columns), jnp.bfloat16),
+            pltpu.VMEM((groups, far_size, merged, columns), jnp.bfloat16),
+            dma((far_size,)), dma((far_size,)), dma((far_size,)), dma((far_size,)),
+            dma((near_size,)), dma((near_size,)),
+            dma((groups, near_size, far_size)), dma((groups, near_size, far_size)),
+            dma((groups, far_size)), dma((groups, far_size)),
+        ],
+        compiler_params=pltpu.CompilerParams(
+            collective_id=0, has_side_effects=True, vmem_limit_bytes=48 * 1024 * 1024
+        ),
+    )(table, ids, maps)
+
+
+def give_back_kernel(
+    sizes, blocks, own_ids, maps_down, totals,
+    far_in, near_out, near_in, far_ss, far_rs, near_ss, near_rs,
+):
+    near_size, far_size, groups, slots, merged = sizes
+    far, near = position(near_size)
+    rows_here, columns = totals.shape
+    greet(near_size, far_size)
+
+    def far_copy(group, step):
+        there = lax.rem(far + step, far_size)
+        return send(
+            blocks.at[group, there],
+            far_in.at[group, far],
+            far_ss.at[group, step],
+            far_rs.at[group, far],
+            there * near_size + near,
+        )
+
+    def far_arrival(group, there):
+        return send(
+            blocks.at[group, there],
+            far_in.at[group, there],
+            far_ss.at[group, 0],
+            far_rs.at[group, there],
+            there * near_size + near,
+        )
+
+    def near_copy(group, step, there):
+        beside = lax.rem(near + step, near_size)
+        return send(
+            near_out.at[group, there, beside],
+            near_in.at[group, near, there],
+            near_ss.at[group, step, there],
+            near_rs.at[group, step, there],
+            far * near_size + beside,
+        )
+
+    for group in range(groups):
+
+        @pl.loop(0, far_size - 1)
+        def _(index):
+            far_copy(group, line_step(index, far_size)).start()
+
+    totals[...] = jnp.zeros_like(totals)
+
+    def spread(group, index):
+        step = lax.rem(index, far_size)
+        there = lax.rem(far + step, far_size)
+
+        @pl.when(step == 0)
+        def _():
+            far_in[group, far] = blocks[group, far]
+
+        @pl.when(step != 0)
+        def _():
+            far_arrival(group, there).wait_recv()
+
+        targets = maps_down[there][:, group : group + 1]
+        picks = lax.broadcasted_iota(jnp.int32, (near_size * slots, merged), 1) == targets
+        rows = jnp.dot(
+            picks.astype(jnp.float32).astype(jnp.bfloat16), far_in[group, there],
+            preferred_element_type=jnp.float32,
+        ).astype(jnp.bfloat16)
+        near_out[group, there] = rows.reshape(near_size, slots, columns)
+        for step in range(1, near_size):
+            near_copy(group, step, there).start()
+        near_in[group, near, there] = near_out[group, there, near]
+
+    def add_up(group, step):
+        beside = lax.rem(near + near_size - step, near_size)
+
+        @pl.when(step != 0)
+        def _():
+            @pl.loop(0, far_size)
+            def _(there):
+                near_copy(group, step, there).wait_recv()
+
+        targets = own_ids[beside][group : group + 1]
+        hits = lax.broadcasted_iota(jnp.int32, (rows_here, far_size * slots), 0) == targets
+        rows = near_in[group, beside].reshape(far_size * slots, columns)
+        totals[...] += jnp.dot(
+            hits.astype(jnp.float32).astype(jnp.bfloat16), rows, preferred_element_type=jnp.float32
+        )
+
+    for group in range(groups):
+
+        @pl.loop(0, far_size)
+        def _(index):
+            spread(group, index)
+
+    for group in range(groups):
+
+        @pl.loop(0, near_size)
+        def _(step):
+            add_up(group, step)
+
+    for group in range(groups):
+        for step in range(1, far_size):
+            far_copy(group, step).wait_send()
+        for step in range(1, near_size):
+
+            @pl.loop(0, far_size)
+            def _(there):
+                near_copy(group, step, there).wait_send()
+
+
+def give_back(blocks, own_ids, maps_down, rows_here, sizes):
+    near_size, far_size, groups, slots, merged = sizes
+    columns = blocks.shape[-1]
+    dma = pltpu.SemaphoreType.DMA
+    vmem = pl.BlockSpec(memory_space=pltpu.VMEM)
+    return pl.pallas_call(
+        functools.partial(give_back_kernel, sizes),
+        name="give_back_rows",
+        out_shape=jax.ShapeDtypeStruct((rows_here, columns), jnp.float32),
+        in_specs=[vmem] * 3,
+        out_specs=vmem,
+        scratch_shapes=[
+            pltpu.VMEM((groups, far_size, merged, columns), jnp.bfloat16),
+            pltpu.VMEM((groups, far_size, near_size, slots, columns), jnp.bfloat16),
+            pltpu.VMEM((groups, near_size, far_size, slots, columns), jnp.bfloat16),
+            dma((groups, far_size)), dma((groups, far_size)),
+            dma((groups, near_size, far_size)), dma((groups, near_size, far_size)),
+        ],
+        compiler_params=pltpu.CompilerParams(
+            collective_id=1, has_side_effects=True, vmem_limit_bytes=48 * 1024 * 1024
+        ),
+    )(blocks, own_ids, maps_down)
 
 
 def group_step(rows_group, rel_float, group_len):
@@ -97,7 +440,9 @@
     )
 
 
-def placement_of(wanted_row, owners, rows_here, slot_count):
+def placement_of(wanted_row, rows_here, sizes):
+    near_size, far_size, _, slots, merged = sizes
+    owners = near_size * far_size
     request_count = wanted_row.shape[0]
     owner_of = wanted_row // rows_here
     owner_hits = (owner_of[:, None] == jnp.arange(owners, dtype=jnp.int32)[None, :]).astype(
@@ -107,24 +452,22 @@
     earlier = (order[:, None] > order[None, :]).astype(jnp.bfloat16)
     before = jnp.dot(earlier, owner_hits, preferred_element_type=jnp.float32)
     slot_rank = jnp.sum(before * owner_hits.astype(jnp.float32), axis=-1).astype(jnp.int32)
-    slot_flat = owner_of * slot_count + slot_rank
-    matches = slot_flat[:, None] == jnp.arange(owners * slot_count, dtype=jnp.int32)[None, :]
-    slot_ids = jnp.sum(jnp.where(matches, wanted_row[:, None] + 1, 0), axis=0) - 1
-    return (matches.astype(jnp.bfloat16), slot_ids.reshape(owners, slot_count))
-
-
-def accumulate(local_rows, received_rows, totals, counts):
-    flat_rows = received_rows.reshape(local_rows.shape[0], received_rows.shape[-1])
-    positions = jnp.arange(totals.shape[0], dtype=jnp.int32)
-    one_hot = (local_rows[:, None] == positions[None, :]).astype(jnp.bfloat16)
-    totals = totals + contract_first(one_hot, flat_rows)
-    counts = counts + jnp.sum(one_hot, axis=0, dtype=jnp.float32)
-    return (totals, counts)
-
-
-def teams(owners):
-    near_size = 4 if owners % 4 == 0 else 1
-    far_size = owners // near_size
+    plane_of = owner_of // near_size
+    same_plane = (
+        plane_of[:, None] == (jnp.arange(owners, dtype=jnp.int32) // near_size)[None, :]
+    ).astype(jnp.float32)
+    plane_rank = jnp.sum(before * same_plane, axis=-1).astype(jnp.int32)
+    slot_flat = owner_of * slots + slot_rank
+    at_slot = slot_flat[:, None] == jnp.arange(owners * slots, dtype=jnp.int32)[None, :]
+    local_row = wanted_row - owner_of * rows_here
+    slot_ids = jnp.sum(jnp.where(at_slot, local_row[:, None] + 1, 0), axis=0) - 1
+    slot_map = jnp.sum(jnp.where(at_slot, plane_rank[:, None] + 1, 0), axis=0) - 1
+    merged_flat = plane_of * merged + plane_rank
+    matches = merged_flat[:, None] == jnp.arange(far_size * merged, dtype=jnp.int32)[None, :]
+    return (matches.astype(jnp.bfloat16), slot_ids, slot_map)
+
+
+def teams(near_size, far_size):
     near = [[row * near_size + place for place in range(near_size)] for row in range(far_size)]
     far = [[row * near_size + place for row in range(far_size)] for place in range(near_size)]
     return (near, far)
@@ -161,57 +504,63 @@
     owners = lax.axis_size("ent")
     rows_here, columns_here = entities.shape
     rel_count = relations.shape[0]
-    row_base = lax.axis_index("ent") * rows_here
     groups_here = negatives.shape[0]
     group_len = triples.shape[1] // groups_here
     request_count = 2 * group_len + negatives.shape[1]
-    slot_count = 8 * ((request_count + 3 * owners - 1) // (3 * owners))
+    slots = 8 * ((request_count + 3 * owners - 1) // (3 * owners))
+    near_size = 4 if owners % 4 == 0 else 1
+    far_size = owners // near_size
+    merged = near_size * slots
+    sizes = (near_size, far_size, groups_here, slots, merged)
     ent_low = entities.astype(jnp.bfloat16)
     head_ids = triples[0].reshape(groups_here, group_len)
     tail_ids = triples[2].reshape(groups_here, group_len)
     wanted = jnp.concatenate([head_ids, tail_ids, negatives], axis=1)
     placed = [
-        placement_of(wanted[index], owners, rows_here, slot_count) for index in range(groups_here)
+        placement_of(wanted[index], rows_here, sizes) for index in range(groups_here)
     ]
-    near, far = teams(owners)
+    near, far = teams(near_size, far_size)
     near_ids = lax.all_gather(triples[1], "ent", axis_index_groups=near, tiled=True)
-    slot_ids = jnp.stack([slots for _, slots in placed], axis=1)
-    received = lax.all_to_all(slot_ids, "ent", split_axis=0, concat_axis=0, tiled=True)
-    local_rows = [received[:, index].reshape(-1) - row_base for index in range(groups_here)]
-    looked_up = [
-        jnp.take(ent_low, rows, axis=0, mode="clip").reshape(
-            owners, slot_count, columns_here
-        )
-        for rows in local_rows
-    ]
-    arrived = exchange(looked_up)
+    slot_ids = jnp.stack([ids for _, ids, _ in placed])
+    slot_ids = slot_ids.reshape(groups_here, far_size, near_size, slots).transpose(1, 2, 0, 3)
+    slot_ids = jnp.pad(
+        slot_ids, ((0, 0), (0, 0), (0, 8 - groups_here), (0, 128 - slots)), constant_values=-1
+    )
+    slot_maps = jnp.stack([maps for _, _, maps in placed])
+    slot_maps = slot_maps.reshape(groups_here, far_size, near_size * slots).transpose(1, 0, 2)
+    slot_maps = jnp.pad(
+        slot_maps, ((0, 0), (0, 8 - groups_here), (0, 0)), constant_values=-1
+    )
+    arrived, own_ids, line_maps = fetch(ent_low, slot_ids, slot_maps, sizes)
+    own_ids = own_ids[..., :slots].transpose(0, 2, 1, 3).reshape(
+        near_size, 8, far_size * slots
+    )
+    maps_down = line_maps.transpose(0, 2, 1)
     rel_float = rounded(jnp.take(relations, triples[1], axis=0, mode="clip")).astype(jnp.float32)
     outgoing, rel_rows = [], []
     for index in range(groups_here):
         matches = placed[index][0]
         rows_group = jnp.dot(
             matches,
-            arrived[index].reshape(owners * slot_count, columns_here),
+            arrived[index].reshape(far_size * merged, columns_here),
             preferred_element_type=jnp.float32,
         ).astype(jnp.bfloat16)
         grads, rel_row = group_step(
             rows_group, rel_float[index * group_len : (index + 1) * group_len], group_len
         )
-        sent = (
+        outgoing.append(
             contract_first(matches, grads)
             .astype(jnp.bfloat16)
-            .reshape(owners, slot_count, columns_here)
-        )
-        if index + 1 < groups_here:
-            sent, arrived[index + 1] = lax.optimization_barrier((sent, arrived[index + 1]))
-        outgoing.append(sent)
+            .reshape(far_size, merged, columns_here)
+        )
         rel_rows.append(rel_row)
+    totals = give_back(jnp.stack(outgoing), own_ids, maps_down, rows_here, sizes)
     rel_grad = sum_relations(jnp.concatenate(rel_rows, axis=0), near_ids, rel_count, near, far)
-    returned = exchange(outgoing)
-    totals = jnp.zeros((rows_here, columns_here), jnp.float32)
-    counts = jnp.zeros((rows_here,), jnp.float32)
-    for index in range(groups_here):
-        totals, counts = accumulate(local_rows[index], returned[index], totals, counts)
+    positions = jnp.arange(rows_here, dtype=jnp.int32)
+    flat_ids = own_ids[:, :groups_here].reshape(-1)
+    counts = jnp.sum(
+        (flat_ids[:, None] == positions[None, :]).astype(jnp.bfloat16), axis=0, dtype=jnp.float32
+    )
     weight = REG_WEIGHT * (buckets.astype(jnp.float32) + 1.0) * counts
     totals = totals + weight[:, None] * 3.0 * entities * jnp.abs(entities)
     ent_squares = jnp.sum(totals * totals, axis=-1)

time: 416 us -> 454 us (1.091)
  Pallas kernels: 0 us -> 267 us
  waiting for transfers between devices: 189 us -> 25.4 us
  starting transfers between devices: 30.4 us -> 4.72 us
  local copies, waits for them, and re-layouts: 58.8 us -> 34.2 us
  matrix products: 50.1 us -> 30.8 us
    pallas_call x0 -> x2, Pallas kernels: none -> 267 us  [the longest x1 153 us: give_back(): pl.pallas_call(functools.partial(give_back_kernel, sizes), name='give_bac...]
    all_to_all x5 -> x0, waiting for transfers between devices: 150 us -> none  [the longest x4 148 us: exchange(): lax.all_to_all(block, 'ent', split_axis=0, concat_axis=0, tiled=True)]
    all_to_all x5 -> x0, starting transfers between devices: 26.7 us -> none  [the longest x4 20.1 us: exchange(): lax.all_to_all(block, 'ent', split_axis=0, concat_axis=0, tiled=True)]
    dot_general x9 -> x7, matrix products: 37.3 us -> 16.3 us  [contract_first(): lax.dot_general(former, latter, (((0,), (0,)), ((), ())), preferred_eleme...]
    gather x2 -> x0, local copies, waits for them, and re-layouts: 18.4 us -> none  [per_device(): jnp.take(ent_low, rows, axis=0, mode='clip')]
    unnamed x35 -> x57, local copies, waits for them, and re-layouts: 12.9 us -> 1.62 us
    reduce_scatter x1, waiting for transfers between devices: 33 us -> 25.4 us  [sum_relations(): lax.psum_scatter(part, 'ent', scatter_dimension=0, axis_index_groups=far,...]
    all_to_all x1, waiting for transfers between devices: 5.89 us -> 0.01 us  [sum_relations(): lax.all_to_all(tiles, 'ent', split_axis=0, concat_axis=0, axis_index_grou...]
  transfers between devices with their start and end apart: 8 -> 3, of which waited for: 7 -> 1; matrix products, arithmetic and copies ran while one was open for 17% -> 5% of each run, Pallas kernels for 0% -> 34%
where the time goes in v1:
time: 454 us; the launch traced here: 447 us
  Pallas kernels  267 us (59%)
  other arithmetic  48.3 us (11%)
  local copies, waits for them, and re-layouts  34.2 us (8%)
  matrix products  30.8 us (7%)
  waiting for transfers between devices  25.4 us (6%)
  blocking collectives  20.6 us (5%)
  between operations  15.3 us (3%)
  starting transfers between devices  4.72 us (1%)
    pallas_call x1, Pallas kernels, give_back(): pl.pallas_call(functools.partial(give_back_kernel, sizes), name='give_bac...  153 us
    pallas_call x1, Pallas kernels, fetch(): pl.pallas_call(functools.partial(fetch_kernel, sizes), name='fetch_rows',...  114 us
    reduce_scatter x1, waiting for transfers between devices, sum_relations(): lax.psum_scatter(part, 'ent', scatter_dimension=0, axis_index_groups=far,...  25.4 us
    dot_general x7, matrix products, contract_first(): lax.dot_general(former, latter, (((0,), (0,)), ((), ())), preferred_eleme...  16.3 us
    sub x2, other arithmetic, adagrad(): return table - grad * scale[:, None]  15.3 us
    convert_element_type x1, local copies, waits for them, and re-layouts, sum_relations(): whole.transpose(0, 2, 1, 3).reshape(rel_count, columns).astype(jnp.float32)  12 us
  transfers between devices with their start and end apart: 3, of which 1 were waited for; matrix products, arithmetic and copies ran while one was open for 5% of the time, Pallas kernels for 34%

profile of v1, /device:TPU:13, one launch (start us, length us, event | category | flops | bytes accessed | tf_op | source)
XLA Modules:
  0.0 446.5 jit_solution(15066513837531090715)
XLA Ops:
  12.7 5.4 %gather_fusion = bf16[512,512]{1,0:T(8,128)(2,1)S(1)} fusion(f32[4096,512]{1,0:T(8,128)} %param.10, s32[1024]{0:T(1024)S(1)} %pad_clamp_fusion), kind=kCustom, calls=%fused_computation | custom fusion | bytes 1050624 | tf_op jit(solution)/shard_map/jit(_take)/gather | solution.py:539
  19.2 2.5 convert_element_type.212.table
  21.7 114.5 %fetch_rows.1 = (bf16[2,4,512,512]{3,2,1,0:T(8,128)(2,1)}, s32[4,4,8,128]{3,2,1,0:T(8,128)S(1)}, s32[4,8,512]{2,1,0:T(8,128)S(1)}) custom-call(bf16[2048,512]{1,0:T(8,128)(2,1)S(1)} %convert_element_type.212.table, s32[4,4,8,128]{3,2,1,0:T(8,128)S(1)} %pad.8.ids, s32[4,8,512]{2,1,0:T(8,128)S(1)} %pad.9.maps), custom_call_target="tpu_custom_call" | custom-call | tf_op jit(solution)/shard_map/fetch_rows/pallas_call | solution.py:245
  136.1 3.8 fusion.81
  140.0 2.2 fusion.18
  144.1 4.2 all_gather.18
  152.3 3.7 fusion.17
  160.1 2.5 all_gather.17
  165.2 2.2 convolution_add_fusion.3
  167.4 2.3 multiply_add_fusion.2
  175.8 4.5 %all-to-all-start = ((bf16[4,512,128]{2,1,0:T(8,128)(2,1)}), bf16[4,512,128]{2,1,0:T(8,128)(2,1)S(1)}, u32[]{:S(2)}, u32[]{:S(2)}) async-start(bf16[4,512,128]{2,1,0:T(8,128)(2,1)} %maximum_bitcast_fusion), calls=%async_computation | async-start | bytes 1048576 | tf_op jit(solution)/shard_map/all_to_all | solution.py:480
  180.2 8.8 %all-gather = s32[1,2048]{1,0:T(1,128)S(1)} all-gather(s32[1,512]{1,0:T(1,128)S(1)} %get-tuple-element.64), channel_id=2, replica_groups={{0,2,4,6},{8,10,12,14},{16,18,20,22},{24,26,28,30},{1,3,5,7},{9,11,13,1..., dimensions={1}, use_global_device_ids=true | all-gather | bytes 10240 | tf_op jit(solution)/shard_map/all_gather | solution.py:523
  189.0 10.2 %fusion.8 = bf16[4096,128]{1,0:T(8,128)(2,1)} fusion(bf16[2048,128]{1,0:T(8,128)(2,1)S(1)} %bitcast.125, s32[2048]{0:T(1024)S(1)} %bitcast.138), kind=kOutput, calls=%fused_computation.22 | convolution fusion | flops 2156396544 | bytes 1581056 | tf_op jit(solution)/shard_map/dot_general | solution.py:47
  199.5 25.4 %reduce-scatter.2.cloned.1.call-done = bf16[1024,128]{1,0:T(8,128)(2,1)} async-done(((bf16[4096,128]{1,0:T(8,128)(2,1)}), bf16[1024,128]{1,0:T(8,128)(2,1)}) %reduce-scatter.2.cloned.1.call-update) | async-done | bytes 262160 | tf_op jit(solution)/shard_map/reduce_scatter | solution.py:489
  233.5 3.0 fusion.13
  238.6 2.4 pad_maximum_fusion.blocks
  241.0 152.6 %give_back_rows.1 = f32[2048,512]{1,0:T(8,128)S(1)} custom-call(bf16[2,4,512,512]{3,2,1,0:T(8,128)(2,1)} %pad_maximum_fusion.blocks, s32[4,8,512]{2,1,0:T(8,128)S(1)} %bitcast.82, s32[4,512,8]{2,1,0:T(8,128)S(1)} %bitcast.80), custom_call_target="tpu_custom_call" | custom-call | tf_op jit(solution)/shard_map/give_back_rows/pallas_call | solution.py:383
  393.6 4.0 convert_reduce_fusion
  399.0 3.9 multiply_reduce_fusion
  403.1 5.1 %all-reduce.2 = (f32[2048]{0:T(1024)S(1)}, f32[4096]{0:T(1024)S(1)}) all-reduce(f32[2048]{0:T(1024)S(1)} %multiply_reduce_fusion.1, f32[4096]{0:T(1024)S(1)} %bitcast.127), channel_id=1, replica_groups=mesh['ent'=16,'dim'=2] {'dim'}, use_global_device_ids=true, to_apply=%region_14.15 | all-reduce | flops 6144 | bytes 49152 | tf_op jit(solution)/shard_map/psum | solution.py:567
  408.2 5.7 %multiply_subtract_fusion = f32[2048,512]{1,0:T(8,128)} fusion(f32[2048,512]{1,0:T(8,128)} %param.7, f32[2048,512]{1,0:T(8,128)} %copy-done, f32[2048]{0:T(1024)S(1)} %rsqrt_multiply_fusion.1, f32[2048]{0:T(1024)S(1)} %multiply_multiply_fusion), kind=kLoop, calls=%fused_computation.24 | loop fusion | flops 6291456 | bytes 12599296 | tf_op jit(solution)/shard_map/sub | solution.py:500
  413.9 3.7 convert_element_type.263
  417.6 12.0 %copy.126 = f32[4,1024,4,128]{3,2,1,0:T(4,128)} copy(f32[4,1024,4,128]{3,1,2,0:T(8,128)} %bitcast.83) | data formatting | bytes 16777216 | tf_op jit(solution)/shard_map/convert_element_type | solution.py:494
  429.6 9.6 %fusion.3 = f32[4096,512]{1,0:T(8,128)} fusion(f32[4096,512]{1,0:T(8,128)} %param.10, f32[512,8,4,128]{3,2,1,0:T(4,128)} %bitcast.84, f32[4096]{0:T(1024)S(1)} %rsqrt_multiply_fusion), kind=kLoop, calls=%fused_computation.8 | loop fusion | flops 4194304 | bytes 25182208 | tf_op jit(solution)/shard_map/sub | solution.py:500
  (151 shorter events, 37.1 us)
Async XLA Ops:
  9.5 130.4 %copy-start.21 = (s32[768]{0:T(1024)}, s32[768]{0:T(1024)S(1)}, u32[]{:S(2)}) copy-start(s32[768]{0:T(1024)S(1)} %get-tuple-element.71) | copy-start | bytes 9220
  11.1 141.2 %copy-start.23 = (s32[768]{0:T(1024)}, s32[768]{0:T(1024)S(1)}, u32[]{:S(2)}) copy-start(s32[768]{0:T(1024)S(1)} %get-tuple-element.65) | copy-start | bytes 9220
  142.4 8.6 %copy-start.4 = (bf16[256,4,2,64]{0,3,2,1:T(8,128)(2,1)}, bf16[256,4,2,64]{0,3,2,1:T(8,128)(2,1)S(1)}, u32[]{:S(2)}) copy-start(bf16[256,4,2,64]{0,3,2,1:T(8,128)(2,1)S(1)} %pad_maximum_fusion.7) | copy-start | bytes 786436
  142.9 5.5 %copy-start.9 = (bf16[256,4,2,64]{0,3,2,1:T(8,128)(2,1)}, bf16[256,4,2,64]{0,3,2,1:T(8,128)(2,1)S(1)}, u32[]{:S(2)}) copy-start(bf16[256,4,2,64]{0,3,2,1:T(8,128)(2,1)S(1)} %pad_maximum_fusion.8) | copy-start | bytes 786436
  148.6 3.7 copy-start.6
  165.1 5.7 %copy-start.14 = (f32[256,512]{0,1:T(8,128)S(1)}, f32[256,512]{0,1:T(8,128)}, u32[]{:S(2)}) copy-start(f32[256,512]{0,1:T(8,128)} %convolution_add_fusion.1) | copy-start | bytes 1572868
  175.8 13.3 %all-to-all-start = ((bf16[4,512,128]{2,1,0:T(8,128)(2,1)}), bf16[4,512,128]{2,1,0:T(8,128)(2,1)S(1)}, u32[]{:S(2)}, u32[]{:S(2)}) async-start(bf16[4,512,128]{2,1,0:T(8,128)(2,1)} %maximum_bitcast_fusion), calls=%async_computation | async-start | bytes 1048576 | tf_op jit(solution)/shard_map/all_to_all | solution.py:480
  180.2 44.7 %reduce-scatter.2.cloned.1.call-start = ((), (), s32[]{:S(2)}) async-start(), calls=%async_computation.2 | async-start | bytes 1310720 | tf_op jit(solution)/shard_map/reduce_scatter | solution.py:489
  199.2 33.1 %copy-start.5 = (bf16[256,4,2,64]{0,3,2,1:T(8,128)(2,1)S(1)}, bf16[256,4,2,64]{0,3,2,1:T(8,128)(2,1)}, u32[]{:S(2)}) copy-start(bf16[256,4,2,64]{0,3,2,1:T(8,128)(2,1)} %copy-done.4) | copy-start | bytes 786436
  199.2 33.1 %copy-start.7 = (bf16[256,512]{1,0:T(8,128)(2,1)S(1)}, bf16[256,512]{1,0:T(8,128)(2,1)}, u32[]{:S(2)}) copy-start(bf16[256,512]{1,0:T(8,128)(2,1)} %copy-done.6) | copy-start | bytes 786436
  199.3 199.8 %all-gather.4.cloned.1.call-start = ((), (), s32[]{:S(2)}) async-start(), calls=%async_computation.3 | async-start | bytes 4456448 | tf_op jit(solution)/shard_map/all_gather | solution.py:492
  224.9 7.7 %copy-start.8 = (bf16[256,512]{1,0:T(8,128)(2,1)S(1)}, bf16[256,512]{1,0:T(8,128)(2,1)}, u32[]{:S(2)}) copy-start(bf16[256,512]{1,0:T(8,128)(2,1)} %fusion.45) | copy-start | bytes 786436
  225.3 7.6 %copy-start.10 = (bf16[256,4,2,64]{0,3,2,1:T(8,128)(2,1)S(1)}, bf16[256,4,2,64]{0,3,2,1:T(8,128)(2,1)}, u32[]{:S(2)}) copy-start(bf16[256,4,2,64]{0,3,2,1:T(8,128)(2,1)} %copy-done.9) | copy-start | bytes 786436
  226.5 6.7 %copy-start.12 = (bf16[256,4,2,64]{0,3,2,1:T(8,128)(2,1)S(1)}, bf16[256,4,2,64]{0,3,2,1:T(8,128)(2,1)}, u32[]{:S(2)}) copy-start(bf16[256,4,2,64]{0,3,2,1:T(8,128)(2,1)} %copy-done.11) | copy-start | bytes 786436
  228.3 5.1 %copy-start.24 = (s32[768]{0:T(1024)S(1)}, s32[768]{0:T(1024)}, u32[]{:S(2)}) copy-start(s32[768]{0:T(1024)} %copy-done.23) | copy-start | bytes 9220
  233.5 3.1 copy-start.16
  233.5 3.1 copy-start.17
  233.5 3.1 copy-start.22
  241.0 156.7 %copy-start.19 = (s32[2048]{0:T(1024)S(1)}, s32[2048]{0:T(1024)}, u32[]{:S(2)}) copy-start(s32[2048]{0:T(1024)} %param.9) | copy-start | bytes 24580
  241.0 156.8 %copy-start.1 = (f32[2048,512]{1,0:T(8,128)S(1)}, f32[2048,512]{1,0:T(8,128)}, u32[]{:S(2)}) copy-start(f32[2048,512]{1,0:T(8,128)} %param.7) | copy-start | bytes 12582916
  393.6 4.1 copy-start
  399.0 9.2 %copy-start.20 = (f32[2048]{0:T(1024)S(1)}, f32[2048]{0:T(1024)}, u32[]{:S(2)}) copy-start(f32[2048]{0:T(1024)} %param.8) | copy-start | bytes 24580
  408.2 5.7 %copy-start.2 = (bf16[16384,128]{1,0:T(8,128)(2,1)S(1)}, bf16[16384,128]{1,0:T(8,128)(2,1)}, u32[]{:S(2)}) copy-start(bf16[16384,128]{1,0:T(8,128)(2,1)} %all-gather.4.cloned.1.call-done) | copy-start | bytes 12582916
  417.6 12.0 %copy-start.18 = (f32[4096]{0:T(1024)S(1)}, f32[4096]{0:T(1024)}, u32[]{:S(2)}) copy-start(f32[4096]{0:T(1024)} %param.11) | copy-start | bytes 49156
  (4 other events, 5.6 us)
Sparse Core Ops, SparseCore 0:
  199.4 25.4 reduce-scatter.1
  227.6 137.6 all-gather.3

commit v2 on v0

v2 whole, which is shorter than its diff:
```python
import functools

import jax
import jax.numpy as jnp
from jax import lax
from jax.experimental import pallas as pl
from jax.experimental.pallas import tpu as pltpu
from jax.sharding import PartitionSpec as P

RANK = 512
BLK = 64


LEARN_RATE = 0.1
REG_WEIGHT = 0.01
MESH = pl.DeviceIdType.MESH
VMEM_LIMIT = 60 * 1024 * 1024


def contract_first(former, latter):
    return lax.dot_general(
        former, latter, (((0,), (0,)), ((), ())), preferred_element_type=jnp.float32
    )


def contract_last(former, latter):
    return lax.dot_general(
        former, latter, (((1,), (1,)), ((), ())), preferred_element_type=jnp.float32
    )


def position(near_size):
    me = lax.axis_index("ent")
    return lax.div(me, near_size), lax.rem(me, near_size)


def greet(near_size, far_size):
    far, near = position(near_size)
    parts = lax.axis_size("dim")
    barrier = pltpu.get_barrier_semaphore()
    for step in range(1, parts):
        peer = lax.rem(lax.axis_index("dim") + step, parts)
        pl.semaphore_signal(barrier, inc=1, device_id={"dim": peer}, device_id_type=MESH)
    for step in range(1, near_size):
        peer = far * near_size + lax.rem(near + step, near_size)
        pl.semaphore_signal(barrier, inc=1, device_id={"ent": peer}, device_id_type=MESH)
    for step in range(1, far_size):
        peer = lax.rem(far + step, far_size) * near_size + near
        pl.semaphore_signal(barrier, inc=1, device_id={"ent": peer}, device_id_type=MESH)
    pl.semaphore_wait(barrier, near_size + far_size + parts - 3)


def send(source, target, send_sem, recv_sem, peer, axis="ent"):
    return pltpu.make_async_remote_copy(
        src_ref=source,
        dst_ref=target,
        send_sem=send_sem,
        recv_sem=recv_sem,
        device_id={axis: peer},
        device_id_type=MESH,
    )


def line_step(index, far_size):
    return jnp.where(
        index == far_size - 1, 0, 1 + lax.rem(far_size // 2 - 1 + index, far_size - 1)
    )


def one_hot(condition):
    return condition.astype(jnp.float32).astype(jnp.bfloat16)


def dot(former, latter):
    return jnp.dot(former, latter, preferred_element_type=jnp.float32)


def swapped(values):
    return pltpu.roll(values, BLK, 1)


def spread_parts(values):
    other = swapped(values)
    first = lax.broadcasted_iota(jnp.int32, values.shape, 1) < BLK
    return jnp.where(first, values, other), jnp.where(first, -other, values)


def times(former, parts):
    return former * parts[0] + swapped(former) * parts[1]


def times_conj(former, parts):
    return former * parts[0] - swapped(former) * parts[1]


def step_kernel(sizes, refs_in, refs_out, scratch):
    near_size, far_size, groups, slots, merged, group_len, width_neg, rel_count = sizes
    table, ids, maps, place_col, place_row, rel_rows, rel_ids = refs_in
    totals, counts, rel_out = refs_out
    s = scratch
    rows_here, columns = table.shape
    in_kernel_sum = "tiles_in" in s
    far, near = position(near_size)
    parts = lax.axis_size("dim")
    part_here = lax.axis_index("dim")
    greet(near_size, far_size)

    def line_peer(step):
        there = lax.rem(far + step, far_size)
        return there, there * near_size + near

    def near_peer(step):
        there = lax.rem(near + step, near_size)
        return there, far * near_size + there

    def ids_copy(step):
        there, peer = line_peer(step)
        return send(ids.at[there], s["line_ids"].at[far], s["ids_ss"].at[step], s["ids_rs"].at[step], peer)

    def maps_copy(step):
        there, peer = line_peer(step)
        return send(maps.at[there], s["line_maps"].at[far], s["maps_ss"].at[step], s["maps_rs"].at[step], peer)

    def fwd_copy(step):
        there, peer = near_peer(step)
        return send(
            s["line_ids"].at[:, there], s["own_ids"].at[near], s["fwd_ss"].at[step], s["fwd_rs"].at[step], peer
        )

    def rel_ids_copy(step):
        there, peer = near_peer(step)
        return send(rel_ids, s["plane_rel"].at[near], s["rid_ss"].at[step], s["rid_rs"].at[step], peer)

    for step in range(1, far_size):
        ids_copy(step).start()
    for step in range(1, far_size):
        maps_copy(step).start()
    if in_kernel_sum:
        for step in range(1, near_size):
            rel_ids_copy(step).start()
        s["plane_rel"][near] = rel_ids[...]
    s["line_ids"][far] = ids[far]
    s["line_maps"][far] = maps[far]
    for step in range(1, far_size):
        ids_copy(step).wait()
    for step in range(1, near_size):
        fwd_copy(step).start()
    s["own_ids"][near] = s["line_ids"][:, near]
    for step in range(1, near_size):
        fwd_copy(step).wait()
    for step in range(1, far_size):
        maps_copy(step).wait()

    def near_copy(group, step, there):
        beside, peer = near_peer(step)
        return send(
            s["near_out"].at[group, step, there], s["near_in"].at[group, there, near],
            s["near_ss"].at[group, step, there], s["near_rs"].at[group, step, there], peer,
        )

    def look_up(group, index):
        step = lax.rem(index + 1, near_size)
        there = lax.rem(far + line_step(lax.div(index, near_size), far_size), far_size)
        beside = lax.rem(near + step, near_size)
        wanted = jnp.transpose(s["own_ids"][beside, there])[:slots, group : group + 1]
        hits = wanted == lax.broadcasted_iota(jnp.int32, (slots, rows_here), 1)
        found = dot(one_hot(hits), table[...]).astype(jnp.bfloat16)

        @pl.when(step == 0)
        def _():
            s["near_in"][group, there, near] = found

        @pl.when(step != 0)
        def _():
            s["near_out"][group, step, there] = found
            near_copy(group, step, there).start()

    def far_copy(group, there, source):
        return send(
            s["far_out"].at[group, there], s["arrived"].at[group, source],
            s["far_ss"].at[group, there], s["far_rs"].at[group, source], there * near_size + near,
        )

    def merge(group, index):
        there = lax.rem(far + line_step(index, far_size), far_size)
        for step in range(1, near_size):
            near_copy(group, step, there).wait_recv()
        targets = s["line_maps"][there][group : group + 1]
        picks = lax.broadcasted_iota(jnp.int32, (merged, near_size * slots), 0) == targets
        rows = s["near_in"][group, there].reshape(near_size * slots, columns)
        block = dot(one_hot(picks), rows).astype(jnp.bfloat16)

        @pl.when(there == far)
        def _():
            s["arrived"][group, far] = block

        @pl.when(there != far)
        def _():
            s["far_out"][group, there] = block
            far_copy(group, there, far).start()

    def part_copy(group, step):
        peer = lax.rem(part_here + step, parts)
        return send(
            s["part_all"].at[group, part_here], s["part_all"].at[group, part_here],
            s["part_ss"].at[group, step], s["part_rs"].at[group, step], peer, axis="dim",
        )

    def tiles_copy(group, step):
        there, peer = near_peer(step)
        span = pl.ds(group * group_len, group_len)
        return send(
            s["tiles_out"].at[there, span], s["tiles_in"].at[near, span],
            s["tiles_ss"].at[group, step], s["tiles_rs"].at[group, step], peer,
        )

    def give_copy(group, there, source):
        return send(
            s["give_out"].at[group, there], s["give_in"].at[group, source],
            s["give_ss"].at[group, there], s["give_rs"].at[group, source], there * near_size + near,
        )

    lanes = 2 * BLK
    blocks = columns // lanes

    def compute(group):
        for step in range(1, far_size):
            far_copy(group, 0, lax.rem(far + step, far_size)).wait_recv()
        incoming = s["arrived"][group].reshape(far_size * merged, columns)
        request_count = 2 * group_len + width_neg
        rows = s["rows"]
        third = 256 if request_count % 256 == 0 else request_count
        for start in range(0, request_count, third):
            at = place_col[start : start + third, group : group + 1]
            picks = lax.broadcasted_iota(jnp.int32, (third, far_size * merged), 1) == at
            rows[start : start + third] = dot(one_hot(picks), incoming).astype(jnp.bfloat16)
        pos = jnp.zeros((group_len, 1), jnp.float32)
        for block in range(blocks):
            cut = slice(block * lanes, (block + 1) * lanes)
            head = rows[:group_len, cut].astype(jnp.float32)
            tail = rows[group_len : 2 * group_len, cut].astype(jnp.float32)
            rel = spread_parts(rel_rows[group * group_len : (group + 1) * group_len, cut].astype(jnp.float32))
            query = times(head, rel).astype(jnp.bfloat16)
            s["query"][:, cut] = query
            s["probe"][:, cut] = times_conj(tail, rel).astype(jnp.bfloat16)
            pos += jnp.sum(query.astype(jnp.float32) * tail, axis=1, keepdims=True)
        noise = rows[2 * group_len :]
        part = s["part_all"]
        part[group, part_here, :, :width_neg] = contract_last(s["query"][...], noise).astype(jnp.bfloat16)
        part[group, part_here, :, width_neg : 2 * width_neg] = contract_last(
            s["probe"][...], noise
        ).astype(jnp.bfloat16)
        part[group, part_here, :, 2 * width_neg :] = jnp.broadcast_to(pos, (group_len, 128)).astype(
            jnp.bfloat16
        )
        for step in range(1, parts):
            part_copy(group, step).start()
        for step in range(1, parts):
            part_copy(group, step).wait_recv()
        scores = part[group, 0].astype(jnp.float32)
        for other in range(1, parts):
            scores += part[group, other].astype(jnp.float32)
        tail_coef = jax.nn.sigmoid(scores[:, :width_neg]) * (1.0 / width_neg)
        head_coef = jax.nn.sigmoid(scores[:, width_neg : 2 * width_neg]) * (1.0 / width_neg)
        pos_coef = -jax.nn.sigmoid(-scores[:, 2 * width_neg :])
        pos_coef = pos_coef.astype(jnp.bfloat16).astype(jnp.float32)[:, :1]
        grads = s["grads"]
        grads[2 * group_len :] = (
            dot(jnp.transpose(tail_coef).astype(jnp.bfloat16), s["query"][...])
            + dot(jnp.transpose(head_coef).astype(jnp.bfloat16), s["probe"][...])
        ).astype(jnp.bfloat16)
        tail_coef = tail_coef.astype(jnp.bfloat16)
        head_coef = head_coef.astype(jnp.bfloat16)
        for block in range(blocks):
            cut = slice(block * lanes, (block + 1) * lanes)
            head = rows[:group_len, cut].astype(jnp.float32)
            tail = rows[group_len : 2 * group_len, cut].astype(jnp.float32)
            rel = spread_parts(rel_rows[group * group_len : (group + 1) * group_len, cut].astype(jnp.float32))
            noise = rows[2 * group_len :, cut]
            tail_pull = pos_coef * tail + dot(tail_coef, noise)
            head_pull = dot(head_coef, noise)
            head_side = pos_coef * head + head_pull
            grads[:group_len, cut] = times_conj(tail_pull, rel).astype(jnp.bfloat16)
            grads[group_len : 2 * group_len, cut] = times(head_side, rel).astype(jnp.bfloat16)
            rel_grad = times_conj(tail_pull, spread_parts(head)) + times_conj(tail, spread_parts(head_pull))
            span = slice(group * group_len, (group + 1) * group_len)
            if in_kernel_sum:
                per_tile = columns // near_size // lanes
                within = slice((block % per_tile) * lanes, (block % per_tile + 1) * lanes)
                s["tiles_out"][block // per_tile, span, within] = rel_grad.astype(jnp.bfloat16)
            else:
                rel_out[span, cut] = rel_grad.astype(jnp.bfloat16)

        @pl.loop(0, far_size)
        def _(index):
            there = lax.rem(far + line_step(index, far_size), far_size)
            at = place_row[group : group + 1] - there * merged
            picks = lax.broadcasted_iota(jnp.int32, (merged, request_count), 0) == at
            block = dot(one_hot(picks), grads[...]).astype(jnp.bfloat16)

            @pl.when(there == far)
            def _():
                s["give_in"][group, far] = block

            @pl.when(there != far)
            def _():
                s["give_out"][group, there] = block
                give_copy(group, there, far).start()

        if in_kernel_sum:
            s["tiles_in"][near, group * group_len : (group + 1) * group_len] = s["tiles_out"][
                near, group * group_len : (group + 1) * group_len
            ]
            for step in range(1, near_size):
                tiles_copy(group, step).start()

    def hand_copy(group, step, there):
        beside, peer = near_peer(step)
        return send(
            s["hand_out"].at[group, there, beside], s["hand_in"].at[group, near, there],
            s["hand_ss"].at[group, step, there], s["hand_rs"].at[group, step, there], peer,
        )

    def spread(group, index):
        there = lax.rem(far + index, far_size)

        @pl.when(index != 0)
        def _():
            give_copy(group, 0, there).wait_recv()

        targets = jnp.transpose(s["line_maps"][there])[:, group : group + 1]
        picks = lax.broadcasted_iota(jnp.int32, (near_size * slots, merged), 1) == targets
        rows = dot(one_hot(picks), s["give_in"][group, there]).astype(jnp.bfloat16)
        s["hand_out"][group, there] = rows.reshape(near_size, slots, columns)
        for step in range(1, near_size):
            hand_copy(group, step, there).start()
        s["hand_in"][group, near, there] = s["hand_out"][group, there, near]

    def add_up(group, step):
        beside = lax.rem(near + near_size - step, near_size)

        @pl.when(step != 0)
        def _():
            @pl.loop(0, far_size)
            def _(there):
                hand_copy(group, step, there).wait_recv()

        @pl.loop(0, far_size)
        def _(there):
            targets = s["own_ids"][beside, there][group : group + 1, :slots]
            hits = lax.broadcasted_iota(jnp.int32, (rows_here, slots), 0) == targets
            totals[...] += dot(one_hot(hits), s["hand_in"][group, beside, there])

    share_len = rel_count // far_size

    def share_copy(step):
        there, peer = line_peer(step)
        span = pl.ds(pl.multiple_of(there * share_len, share_len), share_len)
        return send(
            s["rel_part"].at[span], s["share_in"].at[far], s["share_ss"].at[step], s["share_rs"].at[step], peer
        )

    def rel_block(row, column):
        width = columns // near_size
        return rel_out.at[
            pl.ds(pl.multiple_of(row * share_len, share_len), share_len),
            pl.ds(pl.multiple_of(column * width, width), width),
        ]

    def line_gather(step, source):
        there, peer = line_peer(step)
        block = rel_block(source, near)
        return send(block, block, s["lg_ss"].at[step], s["lg_rs"].at[source], peer)

    def plane_gather(step, row, column):
        there, peer = near_peer(step)
        block = rel_block(row, column)
        return send(block, block, s["pg_ss"].at[step, row], s["pg_rs"].at[column, row], peer)

    def relation_parts():
        for step in range(1, near_size):
            rel_ids_copy(step).wait()
        for group in range(groups):
            for step in range(1, near_size):
                tiles_copy(group, step).wait_recv()
        chunk = 512 if rel_count % 512 == 0 else rel_count

        @pl.loop(0, rel_count // chunk)
        def _(index):
            first = index * chunk
            total = jnp.zeros((chunk, columns // near_size), jnp.float32)
            for beside in range(near_size):
                at = s["plane_rel"][beside][:1] - first
                hits = lax.broadcasted_iota(jnp.int32, (chunk, groups * group_len), 0) == at
                total += dot(one_hot(hits), s["tiles_in"][beside])
            s["rel_part"][pl.ds(pl.multiple_of(first, chunk), chunk)] = total.astype(jnp.bfloat16)

        for step in range(1, far_size):
            share_copy(step).start()

    def relation_share():
        total = s["rel_part"][pl.ds(pl.multiple_of(far * share_len, share_len), share_len)].astype(jnp.float32)
        for step in range(1, far_size):
            share_copy(step).wait_recv()
        for step in range(1, far_size):
            total += s["share_in"][lax.rem(far + step, far_size)].astype(jnp.float32)
        rel_block(far, near)[...] = total.astype(jnp.bfloat16)
        for step in range(1, far_size):
            line_gather(step, far).start()
        for step in range(1, near_size):
            plane_gather(step, far, near).start()

    def relation_forward():
        for step in range(1, far_size):
            row = lax.rem(far + step, far_size)
            line_gather(0, row).wait_recv()
            for beside in range(1, near_size):
                plane_gather(beside, row, near).start()

    def relation_end():
        for step in range(1, near_size):
            there, _ = near_peer(step)

            @pl.loop(0, far_size)
            def _(row):
                plane_gather(0, row, there).wait_recv()

    @pl.loop(0, far_size * near_size)
    def _(index):
        look_up(0, index)

    for group in range(1, groups):

        @pl.loop(0, far_size)
        def _(index):
            @pl.loop(0, near_size)
            def _(part):
                look_up(group, index * near_size + part)

            merge(group - 1, index)

    @pl.loop(0, far_size)
    def _(index):
        merge(groups - 1, index)

    totals[...] = jnp.zeros_like(totals)
    counts[...] = jnp.zeros_like(counts)

    @pl.loop(0, near_size)
    def _(beside):
        @pl.loop(0, far_size)
        def _(there):
            total = jnp.zeros((rows_here, 1), jnp.float32)
            for group in range(groups):
                targets = s["own_ids"][beside, there][group : group + 1, :slots]
                hits = lax.broadcasted_iota(jnp.int32, (rows_here, slots), 0) == targets
                total += jnp.sum(hits.astype(jnp.float32), axis=1, keepdims=True)
            counts[...] += total

    for group in range(groups):
        compute(group)
    for group in range(groups):

        @pl.loop(0, far_size)
        def _(index):
            spread(group, index)

        if in_kernel_sum and group == 0:
            relation_parts()

    if in_kernel_sum:
        relation_share()
    for group in range(groups):
        if in_kernel_sum and group == groups - 1:
            relation_forward()

        @pl.loop(0, near_size)
        def _(step):
            add_up(group, step)

    if in_kernel_sum:
        relation_end()

    for group in range(groups):
        for step in range(1, far_size):
            there = lax.rem(far + step, far_size)
            far_copy(group, there, 0).wait_send()
            give_copy(group, there, 0).wait_send()
        for step in range(1, parts):
            part_copy(group, step).wait_send()
        for step in range(1, near_size):

            @pl.loop(0, far_size)
            def _(there):
                near_copy(group, step, there).wait_send()
                hand_copy(group, step, there).wait_send()

    if in_kernel_sum:
        for step in range(1, near_size):
            for group in range(groups):
                tiles_copy(group, step).wait_send()

            @pl.loop(0, far_size)
            def _(row):
                plane_gather(step, row, near).wait_send()

        for step in range(1, far_size):
            share_copy(step).wait_send()
            line_gather(step, far).wait_send()


def exchange_step(inputs, sizes, collective_id):
    near_size, far_size, groups, slots, merged, group_len, width_neg, rel_count = sizes
    table, ids, maps = inputs[:3]
    rows_here, columns = table.shape
    parts = lax.axis_size("dim")
    dma = pltpu.SemaphoreType.DMA
    low = jnp.bfloat16
    vmem = pl.BlockSpec(memory_space=pltpu.VMEM)
    request_count = 2 * group_len + width_neg
    in_kernel_sum = columns % (2 * BLK * near_size) == 0
    scratch = {
        "line_ids": pltpu.VMEM(ids.shape, jnp.int32),
        "line_maps": pltpu.VMEM(maps.shape, jnp.int32),
        "own_ids": pltpu.VMEM((near_size, far_size) + ids.shape[2:], jnp.int32),
        "near_out": pltpu.VMEM((groups, near_size, far_size, slots, columns), low),
        "near_in": pltpu.VMEM((groups, far_size, near_size, slots, columns), low),
        "far_out": pltpu.VMEM((groups, far_size, merged, columns), low),
        "arrived": pltpu.VMEM((groups, far_size, merged, columns), low),
        "rows": pltpu.VMEM((request_count, columns), low),
        "grads": pltpu.VMEM((request_count, columns), low),
        "query": pltpu.VMEM((group_len, columns), low),
        "probe": pltpu.VMEM((group_len, columns), low),
        "part_all": pltpu.VMEM((groups, parts, group_len, 2 * width_neg + 128), low),
        "give_out": pltpu.VMEM((groups, far_size, merged, columns), low),
        "give_in": pltpu.VMEM((groups, far_size, merged, columns), low),
        "hand_out": pltpu.VMEM((groups, far_size, near_size, slots, columns), low),
        "hand_in": pltpu.VMEM((groups, near_size, far_size, slots, columns), low),
    }
    for name, shape in (
        ("ids", (far_size,)), ("maps", (far_size,)), ("fwd", (near_size,)),
        ("near", (groups, near_size, far_size)), ("far", (groups, far_size)),
        ("part", (groups, parts)), ("give", (groups, far_size)),
        ("hand", (groups, near_size, far_size)),
    ):
        scratch[name + "_ss"] = dma(shape)
        scratch[name + "_rs"] = dma(shape)
    if in_kernel_sum:
        width = columns // near_size
        scratch["plane_rel"] = pltpu.VMEM((near_size, 8, groups * group_len), jnp.int32)
        scratch["tiles_out"] = pltpu.VMEM((near_size, groups * group_len, width), low)
        scratch["tiles_in"] = pltpu.VMEM((near_size, groups * group_len, width), low)
        scratch["rel_part"] = pltpu.VMEM((rel_count, width), low)
        scratch["share_in"] = pltpu.VMEM((far_size, rel_count // far_size, width), low)
        for name, shape in (
            ("rid", (near_size,)), ("tiles", (groups, near_size)), ("share", (far_size,)),
            ("lg", (far_size,)), ("pg", (near_size, far_size)),
        ):
            scratch[name + "_ss"] = dma(shape)
            scratch[name + "_rs"] = dma(shape)
    names = tuple(scratch)
    rel_rows_out = rel_count if in_kernel_sum else groups * group_len

    def kernel(*refs):
        step_kernel(sizes, refs[:7], refs[7:10], dict(zip(names, refs[10:])))

    return pl.pallas_call(
        kernel,
        name="exchange_step",
        out_shape=(
            jax.ShapeDtypeStruct((rows_here, columns), jnp.float32),
            jax.ShapeDtypeStruct((rows_here, 1), jnp.float32),
            jax.ShapeDtypeStruct((rel_rows_out, columns), low),
        ),
        in_specs=[vmem] * 7,
        out_specs=(vmem,) * 3,
        scratch_shapes=list(scratch.values()),
        compiler_params=pltpu.CompilerParams(
            collective_id=collective_id, has_side_effects=True, vmem_limit_bytes=VMEM_LIMIT
        ),
    )(*inputs)


def placement_of(wanted_row, rows_here, sizes):
    near_size, far_size, slots = sizes
    owners = near_size * far_size
    request_count = wanted_row.shape[0]
    owner_of = wanted_row // rows_here
    owner_hits = (owner_of[:, None] == jnp.arange(owners, dtype=jnp.int32)[None, :]).astype(
        jnp.bfloat16
    )
    order = jnp.arange(request_count, dtype=jnp.int32)
    earlier = (order[:, None] > order[None, :]).astype(jnp.bfloat16)
    before = jnp.dot(earlier, owner_hits, preferred_element_type=jnp.float32)
    slot_rank = jnp.sum(before * owner_hits.astype(jnp.float32), axis=-1).astype(jnp.int32)
    plane_of = owner_of // near_size
    same_plane = (
        plane_of[:, None] == (jnp.arange(owners, dtype=jnp.int32) // near_size)[None, :]
    ).astype(jnp.float32)
    plane_rank = jnp.sum(before * same_plane, axis=-1).astype(jnp.int32)
    slot_flat = owner_of * slots + slot_rank
    at_slot = slot_flat[:, None] == jnp.arange(owners * slots, dtype=jnp.int32)[None, :]
    local_row = wanted_row - owner_of * rows_here
    slot_ids = jnp.sum(jnp.where(at_slot, local_row[:, None] + 1, 0), axis=0) - 1
    slot_map = jnp.sum(jnp.where(at_slot, plane_rank[:, None] + 1, 0), axis=0) - 1
    return (plane_of, plane_rank, slot_ids, slot_map)


def teams(near_size, far_size):
    near = [[row * near_size + place for place in range(near_size)] for row in range(far_size)]
    far = [[row * near_size + place for row in range(far_size)] for place in range(near_size)]
    return (near, far)


def sum_relations(rel_rows, near_ids, rel_count, near, far):
    near_size, far_size = len(far), len(near)
    row_count, columns = rel_rows.shape
    tiles = rel_rows.reshape(row_count, near_size, columns // near_size).transpose(1, 0, 2)
    tiles = lax.all_to_all(
        tiles, "ent", split_axis=0, concat_axis=0, axis_index_groups=near, tiled=True
    )
    hits = (near_ids[:, None] == jnp.arange(rel_count, dtype=jnp.int32)[None, :]).astype(
        jnp.bfloat16
    )
    part = contract_first(hits, tiles.reshape(near_size * row_count, columns // near_size)).astype(
        jnp.bfloat16
    )
    share = lax.psum_scatter(
        part, "ent", scatter_dimension=0, axis_index_groups=far, tiled=True
    )
    whole = lax.all_gather(share, "ent", axis=0)
    whole = whole.reshape(far_size, near_size, rel_count // far_size, columns // near_size)
    return whole.transpose(0, 2, 1, 3).reshape(rel_count, columns)


def adagrad(table, state, grad, squares):
    new_state = state + squares / (2 * RANK)
    scale = LEARN_RATE / jnp.sqrt(new_state)
    return table - grad * scale[:, None]


def per_device(entities, ent_state, buckets, relations, rel_state, triples, negatives):
    owners = lax.axis_size("ent")
    rows_here, columns_here = entities.shape
    rel_count = relations.shape[0]
    groups_here, width_neg = negatives.shape
    group_len = triples.shape[1] // groups_here
    request_count = 2 * group_len + width_neg
    slots = 8 * ((request_count + 3 * owners - 1) // (3 * owners))
    near_size = 4 if owners % 4 == 0 else 1
    far_size = owners // near_size
    most = min(near_size * slots, request_count)
    few = min(most, 16 * ((19 * slots + 127) // 128))
    ent_low = entities.astype(jnp.bfloat16)
    head_ids = triples[0].reshape(groups_here, group_len)
    tail_ids = triples[2].reshape(groups_here, group_len)
    wanted = jnp.concatenate([head_ids, tail_ids, negatives], axis=1)
    placed = [
        placement_of(wanted[index], rows_here, (near_size, far_size, slots))
        for index in range(groups_here)
    ]
    plane_of = jnp.stack([each[0] for each in placed])
    plane_rank = jnp.stack([each[1] for each in placed])
    longest = lax.pmax(jnp.max(plane_rank) + 1, ("ent", "dim"))
    slot_ids = jnp.stack([each[2] for each in placed])
    slot_ids = slot_ids.reshape(groups_here, far_size, near_size, slots).transpose(1, 2, 0, 3)
    slot_ids = jnp.pad(
        slot_ids, ((0, 0), (0, 0), (0, 8 - groups_here), (0, 128 - slots)), constant_values=-1
    )
    slot_maps = jnp.stack([each[3] for each in placed])
    slot_maps = slot_maps.reshape(groups_here, far_size, near_size * slots).transpose(1, 0, 2)
    slot_maps = jnp.pad(slot_maps, ((0, 0), (0, 8 - groups_here), (0, 0)), constant_values=-1)
    rel_rows = jnp.take(relations, triples[1], axis=0, mode="clip").astype(jnp.bfloat16)
    rel_ids = jnp.broadcast_to(triples[1][None, :], (8, triples.shape[1]))

    def run(merged, collective_id):
        def branch(plane_of, plane_rank, *inputs):
            place = plane_of * merged + plane_rank
            place_row = jnp.pad(place, ((0, 8 - groups_here), (0, 0)), constant_values=-1)
            sizes = (near_size, far_size, groups_here, slots, merged, group_len, width_neg, rel_count)
            table, ids, maps, rel_rows, rel_ids = inputs
            return exchange_step(
                (table, ids, maps, place_row.T, place_row, rel_rows, rel_ids), sizes, collective_id
            )

        return branch

    operands = (plane_of, plane_rank, ent_low, slot_ids, slot_maps, rel_rows, rel_ids)
    totals, counts, rel_grad = lax.cond(longest <= few, run(few, 0), run(most, 1), *operands)
    if rel_grad.shape[0] != rel_count:
        near, far = teams(near_size, far_size)
        near_ids = lax.all_gather(triples[1], "ent", axis_index_groups=near, tiled=True)
        rel_grad = sum_relations(rel_grad, near_ids, rel_count, near, far)
    rel_grad = rel_grad.astype(jnp.float32)
    weight = REG_WEIGHT * (buckets.astype(jnp.float32) + 1.0) * counts[:, 0]
    totals = totals + weight[:, None] * 3.0 * entities * jnp.abs(entities)
    ent_squares = jnp.sum(totals * totals, axis=-1)
    ent_all, rel_all = lax.psum((ent_squares, jnp.sum(rel_grad * rel_grad, axis=-1)), "dim")
    new_relations = adagrad(relations, rel_state, rel_grad, rel_all)
    new_entities = adagrad(entities, ent_state, totals, ent_all)
    return (new_entities, new_relations)


def solution(mesh):
    placed = (
        P("ent", "dim"),
        P("ent"),
        P("ent"),
        P(None, "dim"),
        P(),
        P(None, "ent"),
        P("ent", None),
    )
    return jax.shard_map(
        per_device,
        mesh=mesh,
        in_specs=placed,
        out_specs=(P("ent", "dim"), P(None, "dim")),
        check_vma=False,
    )
```

time: 416 us -> 301 us (0.72); the launches traced: 409 us -> 299 us
  Pallas kernels: 0 us -> 213 us
  waiting for transfers between devices: 189 us -> 0 us
  matrix products: 50.1 us -> 0.68 us
  local copies, waits for them, and re-layouts: 58.8 us -> 11.1 us
  starting transfers between devices: 30.4 us -> 0 us
  blocking collectives: 20.4 us -> 45.4 us
  other arithmetic: 45.8 us -> 25.8 us
  between operations: 14.8 us -> 2.83 us
    pallas_call x0 -> x1, Pallas kernels: none -> 213 us  [exchange_step(): pl.pallas_call(kernel, name='exchange_step', out_shape=(jax.ShapeDtypeStr...]
    all_to_all x6 -> x0, waiting for transfers between devices: 156 us -> none  [the longest x4 148 us: exchange(): lax.all_to_all(block, 'ent', split_axis=0, concat_axis=0, tiled=True)]
    dot_general x19 -> x0, matrix products: 49.4 us -> none  [the longest x9 37.3 us: contract_first(): lax.dot_general(former, latter, (((0,), (0,)), ((), ())), preferred_eleme...]
    pmax x0 -> x1, blocking collectives: none -> 39.7 us  [per_device(): longest = lax.pmax(jnp.max(plane_rank) + 1, ('ent', 'dim'))]
    reduce_scatter x1 -> x0, waiting for transfers between devices: 33 us -> none  [sum_relations(): lax.psum_scatter(part, 'ent', scatter_dimension=0, axis_index_groups=far,...]
    all_to_all x6 -> x0, starting transfers between devices: 30.1 us -> none  [the longest x4 20.1 us: exchange(): lax.all_to_all(block, 'ent', split_axis=0, concat_axis=0, tiled=True)]
    gather x3 -> x1, local copies, waits for them, and re-layouts: 23.8 us -> 5.36 us  [per_device(): jnp.take(relations, triples[1], axis=0, mode='clip').astype(jnp.bfloat16)]
    convert_element_type x7 -> x2, local copies, waits for them, and re-layouts: 15.3 us -> 0.01 us  [placement_of(): plane_rank = jnp.sum(before * same_plane, axis=-1).astype(jnp.int32)]
  transfers between devices with their start and end apart: 8 -> 0, of which waited for: 7 -> 0; matrix products, arithmetic and copies ran while one was open for 17% -> 0% of each run, Pallas kernels for 0% -> 0%
where the time goes in v2:
time: 301 us; the launch traced here: 299 us
  Pallas kernels  213 us (71%)
  blocking collectives  45.4 us (15%)
  other arithmetic  25.8 us (9%)
  local copies, waits for them, and re-layouts  11.1 us (4%)
    pallas_call x1, Pallas kernels, exchange_step(): pl.pallas_call(kernel, name='exchange_step', out_shape=(jax.ShapeDtypeStr...  213 us
    pmax x1, blocking collectives, per_device(): longest = lax.pmax(jnp.max(plane_rank) + 1, ('ent', 'dim'))  39.7 us
    sub x2, other arithmetic, adagrad(): return table - grad * scale[:, None]  11.5 us

profile of v2, /device:TPU:13, one launch (start us, length us, event | category | flops | bytes accessed | tf_op | source)
XLA Modules:
  0.0 299.3 jit_solution(14520199019047269276)
XLA Ops:
  0.6 0.8 slice_reduce_fusion
  1.5 0.7 constant_dynamic-update-slice_fusion
  2.7 0.4 multiply_reduce_fusion.1
  3.1 0.6 broadcast_add_fusion.4
  3.7 0.6 broadcast_add_fusion.5
  5.7 39.7 %pmax.7 = s32[]{:T(128)} all-reduce(s32[]{:T(128)S(6)} %add.175), channel_id=1, replica_groups=mesh['ent'=16,'dim'=2] {'ent','dim'}, use_global_device_ids=true, to_apply=%region_4.5 | all-reduce | flops 1 | bytes 8 | tf_op jit(solution)/shard_map/pmax | solution.py:664
  46.0 1.5 select_reduce_fusion.1
  47.5 1.5 select_reduce_fusion
  49.1 5.4 %gather_fusion = bf16[512,512]{1,0:T(8,128)(2,1)S(1)} fusion(f32[4096,512]{1,0:T(8,128)} %param.12, s32[1024]{0:T(1024)S(1)} %pad_clamp_fusion), kind=kCustom, calls=%fused_computation | custom fusion | bytes 1050624 | tf_op jit(solution)/shard_map/jit(_take)/gather | solution.py:673
  54.5 2.5 convert_element_type.92
  57.0 216.9 %conditional.1 = ((f32[2048,512]{1,0:T(8,128)}, f32[2048,1]{1,0:T(8,128)}, bf16[4096,512]{1,0:T(8,128)(2,1)})) conditional(s32[]{:T(128)} %convert_element_type.83, (s32[4,4,2,128]{3,2,1,0:T(2,128)S(1)}, s32[4,2,512]{2,1,0:T(2,128)S(1)}, s32[2,768]{1,0:T(2,128)S(1)}, s32[2,768]{1,0:T(2,128)S(1)}, s32[1,512]{1,0:T(1,128)S(1)}, ...), branch_computations={%region_11.12_spmd, %region_12.13_spmd} | conditional | flops 3072 | bytes 305168 | solution.py:689
  57.2 0.6 broadcast_in_dim.69.refs_6_
  57.8 0.6 fusion.17
  58.4 0.6 pad.24.refs_1_
  59.1 0.6 pad.25.refs_2_
  59.7 0.9 copy.14.refs_3_
  60.6 213.0 %exchange_step.5 = (f32[2048,512]{1,0:T(8,128)}, f32[2048,1]{1,0:T(8,128)}, bf16[4096,512]{1,0:T(8,128)(2,1)}) custom-call(bf16[2048,512]{1,0:T(8,128)(2,1)S(1)} %get-tuple-element.94.refs_0_, s32[4,4,8,128]{3,2,1,0:T(8,128)} %pad.24.refs_1_, s32[4,8,512]{2,1,0:T(8,128)} %pad.25.refs_2_, s32[768,8]{1,0:T(8,128)} %copy.14.refs_3_, ...), custom_call_target="tpu_custom_call" | custom-call | tf_op jit(solution)/shard_map/cond/branch_1_fun/exchange_step/pallas_call | solution.py:567
  273.9 1.6 reduce.8
  275.5 4.9 %multiply_reduce_fusion = f32[2048]{0:T(1024)S(1)} fusion(f32[2048,512]{1,0:T(8,128)} %get-tuple-element.119, f32[2048,512]{1,0:T(8,128)} %param.9, f32[2048]{0:T(1024)S(1)} %multiply_multiply_fusion), kind=kLoop, calls=%fused_computation.16 | loop fusion | flops 6289408 | bytes 8404992 | tf_op jit(solution)/shard_map/reduce_sum | solution.py:697
  280.4 0.9 fusion
  281.3 5.7 %all-reduce.6 = (f32[2048]{0:T(1024)S(1)}, f32[4096]{0:T(1024)S(1)}) all-reduce(f32[2048]{0:T(1024)S(1)} %multiply_reduce_fusion, f32[4096]{0:T(1024)S(1)} %fusion), channel_id=1, replica_groups=mesh['ent'=16,'dim'=2] {'dim'}, use_global_device_ids=true, to_apply=%region_14.15 | all-reduce | flops 6144 | bytes 49152 | tf_op jit(solution)/shard_map/psum | solution.py:698
  287.0 5.4 %multiply_subtract_fusion = f32[2048,512]{1,0:T(8,128)} fusion(f32[2048,512]{1,0:T(8,128)} %param.9, f32[2048,512]{1,0:T(8,128)} %get-tuple-element.119, f32[2048]{0:T(1024)S(1)} %rsqrt_multiply_fusion.1, f32[2048]{0:T(1024)S(1)} %multiply_multiply_fusion), kind=kLoop, calls=%fused_computation.15 | loop fusion | flops 6291456 | bytes 12599296 | tf_op jit(solution)/shard_map/sub | solution.py:639
  292.5 0.7 copy-done.1
  293.2 6.1 %fusion.1 = f32[4096,512]{1,0:T(8,128)} fusion(f32[4096,512]{1,0:T(8,128)} %param.12, bf16[4096,512]{1,0:T(8,128)(2,1)S(1)} %copy-done.1, f32[4096]{0:T(1024)S(1)} %rsqrt_multiply_fusion), kind=kLoop, calls=%fused_computation.8 | loop fusion | flops 6291456 | bytes 20987904 | tf_op jit(solution)/shard_map/sub | solution.py:639
  (36 shorter events, 0.6 us)
Async XLA Ops:
  57.0 218.5 %copy-start.3 = (s32[2048]{0:T(1024)S(1)}, s32[2048]{0:T(1024)}, u32[]{:S(2)}) copy-start(s32[2048]{0:T(1024)} %param.11) | copy-start | bytes 24580
  275.5 4.9 %copy-start = (bf16[4096,512]{1,0:T(8,128)(2,1)S(1)}, bf16[4096,512]{1,0:T(8,128)(2,1)}, u32[]{:S(2)}) copy-start(bf16[4096,512]{1,0:T(8,128)(2,1)} %get-tuple-element.118) | copy-start | bytes 12582916
  280.4 6.6 %copy-start.4 = (f32[2048]{0:T(1024)S(1)}, f32[2048]{0:T(1024)}, u32[]{:S(2)}) copy-start(f32[2048]{0:T(1024)} %param.10) | copy-start | bytes 24580
  287.0 5.5 %copy-start.2 = (f32[4096]{0:T(1024)S(1)}, f32[4096]{0:T(1024)}, u32[]{:S(2)}) copy-start(f32[4096]{0:T(1024)} %param.13) | copy-start | bytes 49156
  287.0 6.2 %copy-start.1 = (bf16[4096,512]{1,0:T(8,128)(2,1)S(1)}, bf16[4096,512]{1,0:T(8,128)(2,1)}, u32[]{:S(2)}) copy-start(bf16[4096,512]{1,0:T(8,128)(2,1)} %get-tuple-element.118) | copy-start | bytes 12582916

commit v3 on v2

--- a/solution.py
+++ b/solution.py
@@ -34,9 +34,9 @@
     return lax.div(me, near_size), lax.rem(me, near_size)
 
 
-def greet(near_size, far_size):
+def greet(near_size, far_size, with_parts=True):
     far, near = position(near_size)
-    parts = lax.axis_size("dim")
+    parts = lax.axis_size("dim") if with_parts else 1
     barrier = pltpu.get_barrier_semaphore()
     for step in range(1, parts):
         peer = lax.rem(lax.axis_index("dim") + step, parts)
@@ -93,9 +93,88 @@
     return former * parts[0] - swapped(former) * parts[1]
 
 
+def ids_kernel(sizes, ids, maps, rel_ids, own_ids, line_maps, plane_rel, line_ids, *sems):
+    near_size, far_size = sizes
+    ids_ss, ids_rs, maps_ss, maps_rs, fwd_ss, fwd_rs, rid_ss, rid_rs = sems
+    far, near = position(near_size)
+    greet(near_size, far_size, False)
+
+    def line_peer(step):
+        there = lax.rem(far + step, far_size)
+        return there, there * near_size + near
+
+    def near_peer(step):
+        there = lax.rem(near + step, near_size)
+        return there, far * near_size + there
+
+    def ids_copy(step):
+        there, peer = line_peer(step)
+        return send(ids.at[there], line_ids.at[far], ids_ss.at[step], ids_rs.at[step], peer)
+
+    def maps_copy(step):
+        there, peer = line_peer(step)
+        return send(maps.at[there], line_maps.at[far], maps_ss.at[step], maps_rs.at[step], peer)
+
+    def fwd_copy(step):
+        there, peer = near_peer(step)
+        return send(line_ids.at[:, there], own_ids.at[near], fwd_ss.at[step], fwd_rs.at[step], peer)
+
+    def rel_ids_copy(step):
+        there, peer = near_peer(step)
+        return send(rel_ids, plane_rel.at[near], rid_ss.at[step], rid_rs.at[step], peer)
+
+    for step in range(1, far_size):
+        ids_copy(step).start()
+    for step in range(1, far_size):
+        maps_copy(step).start()
+    for step in range(1, near_size):
+        rel_ids_copy(step).start()
+    plane_rel[near] = rel_ids[...]
+    line_ids[far] = ids[far]
+    line_maps[far] = maps[far]
+    for step in range(1, far_size):
+        ids_copy(step).wait()
+    longest = line_ids[0, 0, 7:8]
+    for there in range(1, far_size):
+        longest = jnp.maximum(longest, line_ids[there, 0, 7:8])
+    for there in range(far_size):
+        for beside in range(near_size):
+            line_ids[there, beside, 7:8] = longest
+    for step in range(1, near_size):
+        fwd_copy(step).start()
+    own_ids[near] = line_ids[:, near]
+    for step in range(1, near_size):
+        fwd_copy(step).wait()
+    for step in range(1, far_size):
+        maps_copy(step).wait()
+    for step in range(1, near_size):
+        rel_ids_copy(step).wait()
+
+
+def share_ids(ids, maps, rel_ids, sizes):
+    near_size, far_size = sizes
+    dma = pltpu.SemaphoreType.DMA
+    vmem = pl.BlockSpec(memory_space=pltpu.VMEM)
+    return pl.pallas_call(
+        functools.partial(ids_kernel, sizes),
+        name="share_ids",
+        out_shape=(
+            jax.ShapeDtypeStruct((near_size, far_size) + ids.shape[2:], jnp.int32),
+            jax.ShapeDtypeStruct(maps.shape, jnp.int32),
+            jax.ShapeDtypeStruct((near_size,) + rel_ids.shape, jnp.int32),
+        ),
+        in_specs=[vmem] * 3,
+        out_specs=(vmem,) * 3,
+        scratch_shapes=[pltpu.VMEM(ids.shape, jnp.int32)]
+        + [dma((far_size,))] * 4
+        + [dma((near_size,))] * 4,
+        compiler_params=pltpu.CompilerParams(collective_id=2, has_side_effects=True),
+    )(ids, maps, rel_ids)
+
+
 def step_kernel(sizes, refs_in, refs_out, scratch):
     near_size, far_size, groups, slots, merged, group_len, width_neg, rel_count = sizes
-    table, ids, maps, place_col, place_row, rel_rows, rel_ids = refs_in
+    table, own_ids, line_maps, place, rel_rows, plane_rel = refs_in
     totals, counts, rel_out = refs_out
     s = scratch
     rows_here, columns = table.shape
@@ -113,44 +192,6 @@
         there = lax.rem(near + step, near_size)
         return there, far * near_size + there
 
-    def ids_copy(step):
-        there, peer = line_peer(step)
-        return send(ids.at[there], s["line_ids"].at[far], s["ids_ss"].at[step], s["ids_rs"].at[step], peer)
-
-    def maps_copy(step):
-        there, peer = line_peer(step)
-        return send(maps.at[there], s["line_maps"].at[far], s["maps_ss"].at[step], s["maps_rs"].at[step], peer)
-
-    def fwd_copy(step):
-        there, peer = near_peer(step)
-        return send(
-            s["line_ids"].at[:, there], s["own_ids"].at[near], s["fwd_ss"].at[step], s["fwd_rs"].at[step], peer
-        )
-
-    def rel_ids_copy(step):
-        there, peer = near_peer(step)
-        return send(rel_ids, s["plane_rel"].at[near], s["rid_ss"].at[step], s["rid_rs"].at[step], peer)
-
-    for step in range(1, far_size):
-        ids_copy(step).start()
-    for step in range(1, far_size):
-        maps_copy(step).start()
-    if in_kernel_sum:
-        for step in range(1, near_size):
-            rel_ids_copy(step).start()
-        s["plane_rel"][near] = rel_ids[...]
-    s["line_ids"][far] = ids[far]
-    s["line_maps"][far] = maps[far]
-    for step in range(1, far_size):
-        ids_copy(step).wait()
-    for step in range(1, near_size):
-        fwd_copy(step).start()
-    s["own_ids"][near] = s["line_ids"][:, near]
-    for step in range(1, near_size):
-        fwd_copy(step).wait()
-    for step in range(1, far_size):
-        maps_copy(step).wait()
-
     def near_copy(group, step, there):
         beside, peer = near_peer(step)
         return send(
@@ -162,7 +203,7 @@
         step = lax.rem(index + 1, near_size)
         there = lax.rem(far + line_step(lax.div(index, near_size), far_size), far_size)
         beside = lax.rem(near + step, near_size)
-        wanted = jnp.transpose(s["own_ids"][beside, there])[:slots, group : group + 1]
+        wanted = jnp.transpose(own_ids[beside, there])[:slots, group : group + 1]
         hits = wanted == lax.broadcasted_iota(jnp.int32, (slots, rows_here), 1)
         found = dot(one_hot(hits), table[...]).astype(jnp.bfloat16)
 
@@ -185,7 +226,7 @@
         there = lax.rem(far + line_step(index, far_size), far_size)
         for step in range(1, near_size):
             near_copy(group, step, there).wait_recv()
-        targets = s["line_maps"][there][group : group + 1]
+        targets = line_maps[there][group : group + 1]
         picks = lax.broadcasted_iota(jnp.int32, (merged, near_size * slots), 0) == targets
         rows = s["near_in"][group, there].reshape(near_size * slots, columns)
         block = dot(one_hot(picks), rows).astype(jnp.bfloat16)
@@ -226,6 +267,8 @@
     def compute(group):
         for step in range(1, far_size):
             far_copy(group, 0, lax.rem(far + step, far_size)).wait_recv()
+        place_col = jnp.transpose(place[:8])
+        place_col = place_col[:, :groups] * merged + place_col[:, groups : 2 * groups]
         incoming = s["arrived"][group].reshape(far_size * merged, columns)
         request_count = 2 * group_len + width_neg
         rows = s["rows"]
@@ -291,22 +334,6 @@
             else:
                 rel_out[span, cut] = rel_grad.astype(jnp.bfloat16)
 
-        @pl.loop(0, far_size)
-        def _(index):
-            there = lax.rem(far + line_step(index, far_size), far_size)
-            at = place_row[group : group + 1] - there * merged
-            picks = lax.broadcasted_iota(jnp.int32, (merged, request_count), 0) == at
-            block = dot(one_hot(picks), grads[...]).astype(jnp.bfloat16)
-
-            @pl.when(there == far)
-            def _():
-                s["give_in"][group, far] = block
-
-            @pl.when(there != far)
-            def _():
-                s["give_out"][group, there] = block
-                give_copy(group, there, far).start()
-
         if in_kernel_sum:
             s["tiles_in"][near, group * group_len : (group + 1) * group_len] = s["tiles_out"][
                 near, group * group_len : (group + 1) * group_len
@@ -314,6 +341,26 @@
             for step in range(1, near_size):
                 tiles_copy(group, step).start()
 
+    def give_blocks(group):
+        @pl.loop(0, far_size)
+        def _(index):
+            there = lax.rem(far + line_step(index, far_size), far_size)
+            at = place[groups + group : groups + group + 1] + (place[group : group + 1] - there) * merged
+            picks = lax.broadcasted_iota(jnp.int32, (merged, s["grads"].shape[0]), 0) == at
+            block = dot(one_hot(picks), s["grads"][...]).astype(jnp.bfloat16)
+
+            @pl.when(there == far)
+            def _():
+                s["give_in"][group, far] = block
+
+            @pl.when(there != far)
+            def _():
+                s["give_out"][group, there] = block
+
+    def give_start(group, index):
+        there = lax.rem(far + line_step(index, far_size), far_size)
+        give_copy(group, there, far).start()
+
     def hand_copy(group, step, there):
         beside, peer = near_peer(step)
         return send(
@@ -322,13 +369,14 @@
         )
 
     def spread(group, index):
-        there = lax.rem(far + index, far_size)
+        offset = jnp.where(index == 0, 0, far_size - line_step(index - 1, far_size))
+        there = lax.rem(far + offset, far_size)
 
         @pl.when(index != 0)
         def _():
             give_copy(group, 0, there).wait_recv()
 
-        targets = jnp.transpose(s["line_maps"][there])[:, group : group + 1]
+        targets = jnp.transpose(line_maps[there])[:, group : group + 1]
         picks = lax.broadcasted_iota(jnp.int32, (near_size * slots, merged), 1) == targets
         rows = dot(one_hot(picks), s["give_in"][group, there]).astype(jnp.bfloat16)
         s["hand_out"][group, there] = rows.reshape(near_size, slots, columns)
@@ -347,39 +395,74 @@
 
         @pl.loop(0, far_size)
         def _(there):
-            targets = s["own_ids"][beside, there][group : group + 1, :slots]
+            targets = own_ids[beside, there][group : group + 1, :slots]
             hits = lax.broadcasted_iota(jnp.int32, (rows_here, slots), 0) == targets
             totals[...] += dot(one_hot(hits), s["hand_in"][group, beside, there])
 
+    def add_up_all(group):
+        @pl.loop(0, near_size)
+        def _(step):
+            add_up(group, step)
+
     share_len = rel_count // far_size
-
-    def share_copy(step):
-        there, peer = line_peer(step)
-        span = pl.ds(pl.multiple_of(there * share_len, share_len), share_len)
+    beside_far = far + 1 - 2 * lax.rem(far, 2)
+    across_far = lax.rem(far + 2, 4)
+    diagonal_far = lax.rem(beside_far + 2, 4)
+    line = lambda there: there * near_size + near
+    near_x = near + 1 - 2 * lax.rem(near, 2)
+    near_y = lax.rem(near + 2, 4)
+    near_xy = lax.rem(near_x + 2, 4)
+    plane = lambda there: far * near_size + there
+
+    def share_rows(row):
+        return pl.ds(pl.multiple_of(row * share_len, share_len), share_len)
+
+    def halve_copy(index):
+        row = beside_far if index == 0 else diagonal_far
         return send(
-            s["rel_part"].at[span], s["share_in"].at[far], s["share_ss"].at[step], s["share_rs"].at[step], peer
+            s["rel_part"].at[share_rows(row)], s["share_in"].at[index],
+            s["halve_ss"].at[index], s["halve_rs"].at[index], line(beside_far),
         )
 
-    def rel_block(row, column):
+    def across_copy():
+        return send(
+            s["share_out"], s["share_in"].at[2], s["double_ss"].at[2], s["double_rs"].at[2], line(across_far)
+        )
+
+    def rel_block(row, column, half=None):
         width = columns // near_size
+        start = row * share_len
+        length = share_len
+        if half is not None:
+            length = share_len // 2
+            start = start + half * length
         return rel_out.at[
-            pl.ds(pl.multiple_of(row * share_len, share_len), share_len),
+            pl.ds(pl.multiple_of(start, length), length),
             pl.ds(pl.multiple_of(column * width, width), width),
         ]
 
-    def line_gather(step, source):
-        there, peer = line_peer(step)
-        block = rel_block(source, near)
-        return send(block, block, s["lg_ss"].at[step], s["lg_rs"].at[source], peer)
-
-    def plane_gather(step, row, column):
-        there, peer = near_peer(step)
+    known_rows = (far, across_far, beside_far, diagonal_far)
+
+    def double_copy(index, row):
+        peer = across_far if index == 0 else beside_far
+        block = rel_block(row, near)
+        return send(block, block, s["double_ss"].at[index], s["double_rs"].at[index], line(peer))
+
+    def pass_copy(row):
+        block = rel_block(row, near)
+        return send(block, block, s["pass_ss"].at[0], s["pass_rs"].at[0], line(beside_far))
+
+    def plane_copy(way, row, column):
+        peer = near_x if way == 0 else near_y
         block = rel_block(row, column)
-        return send(block, block, s["pg_ss"].at[step, row], s["pg_rs"].at[column, row], peer)
+        return send(block, block, s["pg_ss"].at[way, row], s["pg_rs"].at[way, row], plane(peer))
+
+    def relay_copy(way, row, column):
+        peer = near_y if way == 0 else near_x
+        block = rel_block(row, column, way)
+        return send(block, block, s["relay_ss"].at[way, row], s["relay_rs"].at[way, row], plane(peer))
 
     def relation_parts():
-        for step in range(1, near_size):
-            rel_ids_copy(step).wait()
         for group in range(groups):
             for step in range(1, near_size):
                 tiles_copy(group, step).wait_recv()
@@ -390,40 +473,57 @@
             first = index * chunk
             total = jnp.zeros((chunk, columns // near_size), jnp.float32)
             for beside in range(near_size):
-                at = s["plane_rel"][beside][:1] - first
+                at = plane_rel[beside][:1] - first
                 hits = lax.broadcasted_iota(jnp.int32, (chunk, groups * group_len), 0) == at
                 total += dot(one_hot(hits), s["tiles_in"][beside])
             s["rel_part"][pl.ds(pl.multiple_of(first, chunk), chunk)] = total.astype(jnp.bfloat16)
 
-        for step in range(1, far_size):
-            share_copy(step).start()
+        for index in range(2):
+            halve_copy(index).start()
+
+    def part_rows(row):
+        return s["rel_part"][share_rows(row)].astype(jnp.float32)
+
+    def relation_across():
+        halve_copy(1).wait_recv()
+        s["share_out"][...] = (part_rows(across_far) + s["share_in"][1].astype(jnp.float32)).astype(jnp.bfloat16)
+        across_copy().start()
 
     def relation_share():
-        total = s["rel_part"][pl.ds(pl.multiple_of(far * share_len, share_len), share_len)].astype(jnp.float32)
-        for step in range(1, far_size):
-            share_copy(step).wait_recv()
-        for step in range(1, far_size):
-            total += s["share_in"][lax.rem(far + step, far_size)].astype(jnp.float32)
+        halve_copy(0).wait_recv()
+        total = part_rows(far) + s["share_in"][0].astype(jnp.float32)
+        across_copy().wait_recv()
+        total += s["share_in"][2].astype(jnp.float32)
         rel_block(far, near)[...] = total.astype(jnp.bfloat16)
-        for step in range(1, far_size):
-            line_gather(step, far).start()
-        for step in range(1, near_size):
-            plane_gather(step, far, near).start()
-
-    def relation_forward():
-        for step in range(1, far_size):
-            row = lax.rem(far + step, far_size)
-            line_gather(0, row).wait_recv()
-            for beside in range(1, near_size):
-                plane_gather(beside, row, near).start()
+        double_copy(0, far).start()
+        double_copy(1, far).start()
+        for way in range(2):
+            plane_copy(way, far, near).start()
+
+    def relation_known(row):
+        for way in range(2):
+            plane_copy(way, row, near).start()
+
+    def relation_relay(row):
+        plane_copy(0, row, near_x).wait_recv()
+        relay_copy(0, row, near_x).start()
+        plane_copy(1, row, near_y).wait_recv()
+        relay_copy(1, row, near_y).start()
 
     def relation_end():
-        for step in range(1, near_size):
-            there, _ = near_peer(step)
-
-            @pl.loop(0, far_size)
-            def _(row):
-                plane_gather(0, row, there).wait_recv()
+        for row in known_rows:
+            for way in range(2):
+                relay_copy(way, row, near_xy).wait_recv()
+
+    def count_part(beside):
+        @pl.loop(0, far_size)
+        def _(there):
+            total = jnp.zeros((rows_here, 1), jnp.float32)
+            for group in range(groups):
+                targets = own_ids[beside, there][group : group + 1, :slots]
+                hits = lax.broadcasted_iota(jnp.int32, (rows_here, slots), 0) == targets
+                total += jnp.sum(hits.astype(jnp.float32), axis=1, keepdims=True)
+            counts[...] += total
 
     @pl.loop(0, far_size * near_size)
     def _(index):
@@ -439,47 +539,77 @@
 
             merge(group - 1, index)
 
-    @pl.loop(0, far_size)
-    def _(index):
-        merge(groups - 1, index)
-
     totals[...] = jnp.zeros_like(totals)
     counts[...] = jnp.zeros_like(counts)
 
     @pl.loop(0, near_size)
     def _(beside):
-        @pl.loop(0, far_size)
-        def _(there):
-            total = jnp.zeros((rows_here, 1), jnp.float32)
-            for group in range(groups):
-                targets = s["own_ids"][beside, there][group : group + 1, :slots]
-                hits = lax.broadcasted_iota(jnp.int32, (rows_here, slots), 0) == targets
-                total += jnp.sum(hits.astype(jnp.float32), axis=1, keepdims=True)
-            counts[...] += total
-
-    for group in range(groups):
+        count_part(beside)
+
+    last = groups - 1
+    early = far_size // 2 if groups > 1 else far_size
+
+    @pl.loop(0, early)
+    def _(index):
+        merge(last, index)
+
+    for group in range(last):
         compute(group)
-    for group in range(groups):
-
-        @pl.loop(0, far_size)
-        def _(index):
-            spread(group, index)
-
-        if in_kernel_sum and group == 0:
-            relation_parts()
-
+        if group == 0:
+
+            @pl.loop(early, far_size)
+            def _(index):
+                merge(last, index)
+
+        give_blocks(group)
+        for index in range(far_size - 1):
+            give_start(group, index)
+
+    compute(last)
+    give_blocks(last)
     if in_kernel_sum:
+        relation_parts()
+        give_start(last, 0)
+        for group in range(last):
+
+            @pl.loop(0, far_size)
+            def _(index):
+                spread(group, index)
+
+        relation_across()
+        give_start(last, 1)
         relation_share()
-    for group in range(groups):
-        if in_kernel_sum and group == groups - 1:
-            relation_forward()
-
-        @pl.loop(0, near_size)
-        def _(step):
-            add_up(group, step)
-
-    if in_kernel_sum:
+        give_start(last, 2)
+        for group in range(last):
+            add_up_all(group)
+        spread(last, 0)
+        double_copy(0, across_far).wait_recv()
+        pass_copy(across_far).start()
+        relation_known(across_far)
+        relation_relay(far)
+        double_copy(1, beside_far).wait_recv()
+        relation_known(beside_far)
+        spread(last, 1)
+        pass_copy(diagonal_far).wait_recv()
+        relation_known(diagonal_far)
+        relation_relay(across_far)
+        relation_relay(beside_far)
+        spread(last, 2)
+        spread(last, 3)
+        relation_relay(diagonal_far)
+        add_up_all(last)
         relation_end()
+    else:
+        for index in range(far_size - 1):
+            give_start(last, index)
+        for group in range(groups):
+
+            @pl.loop(0, far_size)
+            def _(index):
+                spread(group, index)
+
+        for group in range(groups):
+            add_up_all(group)
 
     for group in range(groups):
         for step in range(1, far_size):
@@ -499,30 +629,32 @@
         for step in range(1, near_size):
             for group in range(groups):
                 tiles_copy(group, step).wait_send()
-
-            @pl.loop(0, far_size)
-            def _(row):
-                plane_gather(step, row, near).wait_send()
-
-        for step in range(1, far_size):
-            share_copy(step).wait_send()
-            line_gather(step, far).wait_send()
+        for index in range(2):
+            halve_copy(index).wait_send()
+            double_copy(index, far).wait_send()
+        across_copy().wait_send()
+        pass_copy(across_far).wait_send()
+        for row in known_rows:
+            for way in range(2):
+                plane_copy(way, row, near).wait_send()
+                relay_copy(way, row, near).wait_send()
+
+
+def sums_in_kernel(columns, near_size, far_size):
+    return near_size == 4 and far_size == 4 and columns % (2 * BLK * near_size) == 0
 
 
 def exchange_step(inputs, sizes, collective_id):
     near_size, far_size, groups, slots, merged, group_len, width_neg, rel_count = sizes
-    table, ids, maps = inputs[:3]
+    table = inputs[0]
     rows_here, columns = table.shape
     parts = lax.axis_size("dim")
     dma = pltpu.SemaphoreType.DMA
     low = jnp.bfloat16
     vmem = pl.BlockSpec(memory_space=pltpu.VMEM)
     request_count = 2 * group_len + width_neg
-    in_kernel_sum = columns % (2 * BLK * near_size) == 0
+    in_kernel_sum = sums_in_kernel(columns, near_size, far_size)
     scratch = {
-        "line_ids": pltpu.VMEM(ids.shape, jnp.int32),
-        "line_maps": pltpu.VMEM(maps.shape, jnp.int32),
-        "own_ids": pltpu.VMEM((near_size, far_size) + ids.shape[2:], jnp.int32),
         "near_out": pltpu.VMEM((groups, near_size, far_size, slots, columns), low),
         "near_in": pltpu.VMEM((groups, far_size, near_size, slots, columns), low),
         "far_out": pltpu.VMEM((groups, far_size, merged, columns), low),
@@ -538,7 +670,6 @@
         "hand_in": pltpu.VMEM((groups, near_size, far_size, slots, columns), low),
     }
     for name, shape in (
-        ("ids", (far_size,)), ("maps", (far_size,)), ("fwd", (near_size,)),
         ("near", (groups, near_size, far_size)), ("far", (groups, far_size)),
         ("part", (groups, parts)), ("give", (groups, far_size)),
         ("hand", (groups, near_size, far_size)),
@@ -547,14 +678,14 @@
         scratch[name + "_rs"] = dma(shape)
     if in_kernel_sum:
         width = columns // near_size
-        scratch["plane_rel"] = pltpu.VMEM((near_size, 8, groups * group_len), jnp.int32)
         scratch["tiles_out"] = pltpu.VMEM((near_size, groups * group_len, width), low)
         scratch["tiles_in"] = pltpu.VMEM((near_size, groups * group_len, width), low)
         scratch["rel_part"] = pltpu.VMEM((rel_count, width), low)
-        scratch["share_in"] = pltpu.VMEM((far_size, rel_count // far_size, width), low)
+        scratch["share_in"] = pltpu.VMEM((3, rel_count // far_size, width), low)
+        scratch["share_out"] = pltpu.VMEM((rel_count // far_size, width), low)
         for name, shape in (
-            ("rid", (near_size,)), ("tiles", (groups, near_size)), ("share", (far_size,)),
-            ("lg", (far_size,)), ("pg", (near_size, far_size)),
+            ("tiles", (groups, near_size)), ("halve", (2,)), ("double", (3,)), ("pass", (1,)),
+            ("pg", (2, far_size)), ("relay", (2, far_size)),
         ):
             scratch[name + "_ss"] = dma(shape)
             scratch[name + "_rs"] = dma(shape)
@@ -562,7 +693,7 @@
     rel_rows_out = rel_count if in_kernel_sum else groups * group_len
 
     def kernel(*refs):
-        step_kernel(sizes, refs[:7], refs[7:10], dict(zip(names, refs[10:])))
+        step_kernel(sizes, refs[:6], refs[6:9], dict(zip(names, refs[9:])))
 
     return pl.pallas_call(
         kernel,
@@ -572,7 +703,7 @@
             jax.ShapeDtypeStruct((rows_here, 1), jnp.float32),
             jax.ShapeDtypeStruct((rel_rows_out, columns), low),
         ),
-        in_specs=[vmem] * 7,
+        in_specs=[vmem] * 6,
         out_specs=(vmem,) * 3,
         scratch_shapes=list(scratch.values()),
         compiler_params=pltpu.CompilerParams(
@@ -661,31 +792,30 @@
     ]
     plane_of = jnp.stack([each[0] for each in placed])
     plane_rank = jnp.stack([each[1] for each in placed])
-    longest = lax.pmax(jnp.max(plane_rank) + 1, ("ent", "dim"))
     slot_ids = jnp.stack([each[2] for each in placed])
     slot_ids = slot_ids.reshape(groups_here, far_size, near_size, slots).transpose(1, 2, 0, 3)
     slot_ids = jnp.pad(
         slot_ids, ((0, 0), (0, 0), (0, 8 - groups_here), (0, 128 - slots)), constant_values=-1
     )
+    is_last_row = jnp.arange(8, dtype=jnp.int32)[:, None] == 7
+    slot_ids = jnp.where(is_last_row, jnp.max(plane_rank) + 1, slot_ids)
     slot_maps = jnp.stack([each[3] for each in placed])
     slot_maps = slot_maps.reshape(groups_here, far_size, near_size * slots).transpose(1, 0, 2)
     slot_maps = jnp.pad(slot_maps, ((0, 0), (0, 8 - groups_here), (0, 0)), constant_values=-1)
     rel_rows = jnp.take(relations, triples[1], axis=0, mode="clip").astype(jnp.bfloat16)
     rel_ids = jnp.broadcast_to(triples[1][None, :], (8, triples.shape[1]))
 
+    own_ids, line_maps, plane_rel = share_ids(slot_ids, slot_maps, rel_ids, (near_size, far_size))
+    longest = jnp.max(own_ids[:, 0, 7, 0])
+    place = jnp.pad(
+        jnp.concatenate([plane_of, plane_rank]), ((0, 8 - 2 * groups_here), (0, 0)), constant_values=-1
+    )
+
     def run(merged, collective_id):
-        def branch(plane_of, plane_rank, *inputs):
-            place = plane_of * merged + plane_rank
-            place_row = jnp.pad(place, ((0, 8 - groups_here), (0, 0)), constant_values=-1)
-            sizes = (near_size, far_size, groups_here, slots, merged, group_len, width_neg, rel_count)
-            table, ids, maps, rel_rows, rel_ids = inputs
-            return exchange_step(
-                (table, ids, maps, place_row.T, place_row, rel_rows, rel_ids), sizes, collective_id
-            )
-
-        return branch
-
-    operands = (plane_of, plane_rank, ent_low, slot_ids, slot_maps, rel_rows, rel_ids)
+        sizes = (near_size, far_size, groups_here, slots, merged, group_len, width_neg, rel_count)
+        return lambda *inputs: exchange_step(inputs, sizes, collective_id)
+
+    operands = (ent_low, own_ids, line_maps, place, rel_rows, plane_rel)
     totals, counts, rel_grad = lax.cond(longest <= few, run(few, 0), run(most, 1), *operands)
     if rel_grad.shape[0] != rel_count:
         near, far = teams(near_size, far_size)

time: 301 us -> 261 us (0.87)
  blocking collectives: 45.4 us -> 7.32 us
    pmax x1 -> x0, blocking collectives: 39.7 us -> none  [per_device(): longest = lax.pmax(jnp.max(plane_rank) + 1, ('ent', 'dim'))]
    pallas_call x0 -> x1, Pallas kernels: none -> 8.61 us  [share_ids(): pl.pallas_call(functools.partial(ids_kernel, sizes), name='share_ids', ou...]
    pallas_call x1, Pallas kernels: 213 us -> 205 us  [exchange_step(): pl.pallas_call(kernel, name='exchange_step', out_shape=(jax.ShapeDtypeStr...]
where the time goes in v3:
time: 261 us; the launch traced here: 260 us
  Pallas kernels  213 us (82%)
  other arithmetic  25.9 us (10%)
  local copies, waits for them, and re-layouts  9.53 us (4%)
  blocking collectives  7.32 us (3%)
  between operations  2.83 us (1%)
    pallas_call x1, Pallas kernels, exchange_step(): pl.pallas_call(kernel, name='exchange_step', out_shape=(jax.ShapeDtypeStr...  205 us
    sub x2, other arithmetic, adagrad(): return table - grad * scale[:, None]  11.5 us
    pallas_call x1, Pallas kernels, share_ids(): pl.pallas_call(functools.partial(ids_kernel, sizes), name='share_ids', ou...  8.61 us
    psum x1, blocking collectives, per_device(): lax.psum((ent_squares, jnp.sum(rel_grad * rel_grad, axis=-1)), 'dim')  7.32 us
    gather x1, local copies, waits for them, and re-layouts, per_device(): jnp.take(relations, triples[1], axis=0, mode='clip').astype(jnp.bfloat16)  5.36 us

profile of v3, /device:TPU:13, one launch (start us, length us, event | category | flops | bytes accessed | tf_op | source)
XLA Modules:
  0.0 259.9 jit_solution(11129310461768331294)
XLA Ops:
  0.7 0.8 slice_reduce_fusion.1
  1.5 0.7 constant_dynamic-update-slice_fusion
  2.3 0.6 broadcast_in_dim.85.rel_ids
  3.2 0.4 select_reduce_fusion.4
  3.7 0.6 convert_reduce_fusion
  4.3 0.6 convert_reduce_fusion.1
  6.3 1.5 select_reduce_fusion.1
  7.8 1.5 select_reduce_fusion
  9.4 0.7 pad_select_fusion.ids
  10.1 0.6 pad.17.maps
  10.7 8.6 %share_ids.1 = (s32[4,4,8,128]{3,2,1,0:T(8,128)S(1)}, s32[4,8,512]{2,1,0:T(8,128)S(1)}, s32[4,8,512]{2,1,0:T(8,128)S(1)}) custom-call(s32[4,4,8,128]{3,2,1,0:T(8,128)} %pad_select_fusion.ids, s32[4,8,512]{2,1,0:T(8,128)} %pad.17.maps, s32[8,512]{1,0:T(8,128)} %broadcast_in_dim.85.rel_ids), custom_call_target="tpu_custom_call" | custom-call | tf_op jit(solution)/shard_map/share_ids/pallas_call | solution.py:158
  19.3 0.6 slice_reduce_fusion
  20.6 5.4 %gather_fusion = bf16[512,512]{1,0:T(8,128)(2,1)S(1)} fusion(f32[4096,512]{1,0:T(8,128)} %param.12, s32[1024]{0:T(1024)S(1)} %pad_clamp_fusion), kind=kCustom, calls=%fused_computation | custom fusion | bytes 1050624 | tf_op jit(solution)/shard_map/jit(_take)/gather | solution.py:805
  26.0 2.5 convert_element_type.92
  28.5 205.7 %conditional.1 = ((f32[2048,512]{1,0:T(8,128)}, f32[2048,1]{1,0:T(8,128)S(1)}, bf16[4096,512]{1,0:T(8,128)(2,1)})) conditional(s32[]{:T(128)} %convert_element_type.89, (s32[4,768]{1,0:T(4,128)S(1)}, bf16[2048,512]{1,0:T(8,128)(2,1)S(1)}, s32[4,4,8,128]{3,2,1,0:T(8,128)S(1)}, s32[4,8,512]{2,1,0:T(8,128)S(1)}, bf16[512,512]{1,0:T(8,128)(2,1)S(1)}, ...), branch_computations={%region_11.12_spmd, %region_12.13_spmd} | conditional | bytes 36876 | solution.py:819
  28.7 0.6 pad.13.refs_3_
  29.3 204.5 %exchange_step.3 = (f32[2048,512]{1,0:T(8,128)}, f32[2048,1]{1,0:T(8,128)S(1)}, bf16[4096,512]{1,0:T(8,128)(2,1)}) custom-call(bf16[2048,512]{1,0:T(8,128)(2,1)S(1)} %get-tuple-element.45.refs_0_, s32[4,4,8,128]{3,2,1,0:T(8,128)S(1)} %get-tuple-element.46.refs_1_, s32[4,8,512]{2,1,0:T(8,128)S(1)} %get-tuple-element.47.refs_2_, s32[8,768]{1,0:T(8,128)} %pad.13.refs_3_, ...), custom_call_target="tpu_custom_call" | custom-call | tf_op jit(solution)/shard_map/cond/branch_1_fun/exchange_step/pallas_call | solution.py:698
  234.1 0.3 reduce.9
  234.5 4.9 %multiply_reduce_fusion = f32[2048]{0:T(1024)S(1)} fusion(f32[2048,512]{1,0:T(8,128)} %get-tuple-element.75, f32[2048,512]{1,0:T(8,128)} %param.9, f32[2048]{0:T(1024)S(1)} %multiply_multiply_fusion), kind=kLoop, calls=%fused_computation.12 | loop fusion | flops 6289408 | bytes 8404992 | tf_op jit(solution)/shard_map/reduce_sum | solution.py:827
  239.4 0.9 fusion
  240.3 7.3 %all-reduce.4 = (f32[2048]{0:T(1024)S(1)}, f32[4096]{0:T(1024)S(1)}) all-reduce(f32[2048]{0:T(1024)S(1)} %multiply_reduce_fusion, f32[4096]{0:T(1024)S(1)} %fusion), channel_id=1, replica_groups=mesh['ent'=16,'dim'=2] {'dim'}, use_global_device_ids=true, to_apply=%region_14.15 | all-reduce | flops 6144 | bytes 49152 | tf_op jit(solution)/shard_map/psum | solution.py:828
  247.7 5.4 %multiply_subtract_fusion = f32[2048,512]{1,0:T(8,128)} fusion(f32[2048,512]{1,0:T(8,128)} %param.9, f32[2048,512]{1,0:T(8,128)} %get-tuple-element.75, f32[2048]{0:T(1024)S(1)} %rsqrt_multiply_fusion.1, f32[2048]{0:T(1024)S(1)} %multiply_multiply_fusion), kind=kLoop, calls=%fused_computation.11 | loop fusion | flops 6291456 | bytes 12599296 | tf_op jit(solution)/shard_map/sub | solution.py:770
  253.1 0.7 copy-done.1
  253.8 6.1 %fusion.1 = f32[4096,512]{1,0:T(8,128)} fusion(f32[4096,512]{1,0:T(8,128)} %param.12, bf16[4096,512]{1,0:T(8,128)(2,1)S(1)} %copy-done.1, f32[4096]{0:T(1024)S(1)} %rsqrt_multiply_fusion), kind=kLoop, calls=%fused_computation.4 | loop fusion | flops 6291456 | bytes 20987904 | tf_op jit(solution)/shard_map/sub | solution.py:770
  (35 shorter events, 0.6 us)
Async XLA Ops:
  28.5 206.0 %copy-start.3 = (s32[2048]{0:T(1024)S(1)}, s32[2048]{0:T(1024)}, u32[]{:S(2)}) copy-start(s32[2048]{0:T(1024)} %param.11) | copy-start | bytes 24580
  234.5 4.9 %copy-start = (bf16[4096,512]{1,0:T(8,128)(2,1)S(1)}, bf16[4096,512]{1,0:T(8,128)(2,1)}, u32[]{:S(2)}) copy-start(bf16[4096,512]{1,0:T(8,128)(2,1)} %get-tuple-element.74) | copy-start | bytes 12582916
  239.4 8.2 %copy-start.4 = (f32[2048]{0:T(1024)S(1)}, f32[2048]{0:T(1024)}, u32[]{:S(2)}) copy-start(f32[2048]{0:T(1024)} %param.10) | copy-start | bytes 24580
  247.7 5.5 %copy-start.2 = (f32[4096]{0:T(1024)S(1)}, f32[4096]{0:T(1024)}, u32[]{:S(2)}) copy-start(f32[4096]{0:T(1024)} %param.13) | copy-start | bytes 49156
  247.7 6.2 %copy-start.1 = (bf16[4096,512]{1,0:T(8,128)(2,1)S(1)}, bf16[4096,512]{1,0:T(8,128)(2,1)}, u32[]{:S(2)}) copy-start(bf16[4096,512]{1,0:T(8,128)(2,1)} %get-tuple-element.74) | copy-start | bytes 12582916

commit v4 on v3

--- a/solution.py
+++ b/solution.py
@@ -174,10 +174,12 @@
 
 def step_kernel(sizes, refs_in, refs_out, scratch):
     near_size, far_size, groups, slots, merged, group_len, width_neg, rel_count = sizes
-    table, own_ids, line_maps, place, rel_rows, plane_rel = refs_in
-    totals, counts, rel_out = refs_out
+    entities, own_ids, line_maps, place, rel_rows, plane_rel, weights = refs_in
+    totals, ent_squares, rel_out, rel_squares = refs_out
     s = scratch
-    rows_here, columns = table.shape
+    table = s["table"]
+    rows_here, columns = entities.shape
+    table[...] = entities[...].astype(jnp.bfloat16)
     in_kernel_sum = "tiles_in" in s
     far, near = position(near_size)
     parts = lax.axis_size("dim")
@@ -393,11 +395,26 @@
             def _(there):
                 hand_copy(group, step, there).wait_recv()
 
-        @pl.loop(0, far_size)
-        def _(there):
-            targets = own_ids[beside, there][group : group + 1, :slots]
-            hits = lax.broadcasted_iota(jnp.int32, (rows_here, slots), 0) == targets
-            totals[...] += dot(one_hot(hits), s["hand_in"][group, beside, there])
+        if slots % 128 == 0:
+            targets = jnp.concatenate(
+                [own_ids[beside, there][group : group + 1, :slots] for there in range(far_size)], axis=1
+            )
+            rows = s["hand_in"][group, beside].reshape(far_size * slots, columns)
+            chunk = 512 if rows_here % 512 == 0 else rows_here
+
+            @pl.loop(0, rows_here // chunk)
+            def _(index):
+                first = pl.multiple_of(index * chunk, chunk)
+                hits = lax.broadcasted_iota(jnp.int32, (chunk, far_size * slots), 0) == targets - first
+                totals[pl.ds(first, chunk)] += dot(one_hot(hits), rows)
+
+        else:
+
+            @pl.loop(0, far_size)
+            def _(there):
+                targets = own_ids[beside, there][group : group + 1, :slots]
+                hits = lax.broadcasted_iota(jnp.int32, (rows_here, slots), 0) == targets
+                totals[...] += dot(one_hot(hits), s["hand_in"][group, beside, there])
 
     def add_up_all(group):
         @pl.loop(0, near_size)
@@ -515,15 +532,49 @@
             for way in range(2):
                 relay_copy(way, row, near_xy).wait_recv()
 
-    def count_part(beside):
-        @pl.loop(0, far_size)
-        def _(there):
-            total = jnp.zeros((rows_here, 1), jnp.float32)
-            for group in range(groups):
-                targets = own_ids[beside, there][group : group + 1, :slots]
-                hits = lax.broadcasted_iota(jnp.int32, (rows_here, slots), 0) == targets
-                total += jnp.sum(hits.astype(jnp.float32), axis=1, keepdims=True)
-            counts[...] += total
+    span = 256 if rows_here % 256 == 0 else rows_here
+
+    def start_totals(index):
+        first = pl.multiple_of(index * span, span)
+        rows_of = first + lax.broadcasted_iota(jnp.int32, (span, slots), 0)
+        count = jnp.zeros((span, slots), jnp.float32)
+        for beside in range(near_size):
+            for there in range(far_size):
+                for group in range(groups):
+                    targets = own_ids[beside, there][group : group + 1, :slots]
+                    count += (rows_of == targets).astype(jnp.float32)
+        count = jnp.sum(count, axis=1, keepdims=True)
+        weight = jnp.transpose(weights[:, pl.ds(first, span)])[:, :1] * count
+        own = entities[pl.ds(first, span)]
+        totals[pl.ds(first, span)] = weight * own * jnp.abs(own)
+
+    def norm_copy(which, step):
+        peer = lax.rem(part_here + step, parts)
+        held = s["rel_all" if which else "ent_all"].at[part_here]
+        return send(held, held, s["norm_ss"].at[which, step], s["norm_rs"].at[which, step], peer, axis="dim")
+
+    def norm_start(which):
+        values = rel_out if which else totals
+        held = s["rel_all" if which else "ent_all"]
+
+        @pl.loop(0, values.shape[0] // span)
+        def _(index):
+            first = pl.multiple_of(index * span, span)
+            block = values[pl.ds(first, span)].astype(jnp.float32)
+            square = jnp.sum(block * block, axis=1, keepdims=True)
+            held[part_here, :, pl.ds(first, span)] = jnp.transpose(jnp.broadcast_to(square, (span, 8)))
+
+        for step in range(1, parts):
+            norm_copy(which, step).start()
+
+    def norm_end(which):
+        held = s["rel_all" if which else "ent_all"]
+        for step in range(1, parts):
+            norm_copy(which, step).wait()
+        total = held[0]
+        for other in range(1, parts):
+            total += held[other]
+        (rel_squares if which else ent_squares)[...] = total
 
     @pl.loop(0, far_size * near_size)
     def _(index):
@@ -539,12 +590,9 @@
 
             merge(group - 1, index)
 
-    totals[...] = jnp.zeros_like(totals)
-    counts[...] = jnp.zeros_like(counts)
-
-    @pl.loop(0, near_size)
-    def _(beside):
-        count_part(beside)
+    @pl.loop(0, rows_here // span)
+    def _(index):
+        start_totals(index)
 
     last = groups - 1
     early = far_size // 2 if groups > 1 else far_size
@@ -565,51 +613,59 @@
         for index in range(far_size - 1):
             give_start(group, index)
 
+    if last > 0:
+        spread(0, 0)
     compute(last)
-    give_blocks(last)
     if in_kernel_sum:
+        for index in range(1, far_size - 1):
+            if last > 0:
+                spread(0, index)
         relation_parts()
+        give_blocks(last)
         give_start(last, 0)
-        for group in range(last):
-
-            @pl.loop(0, far_size)
-            def _(index):
-                spread(group, index)
-
+        if last > 0:
+            spread(0, far_size - 1)
         relation_across()
+        spread(last, 0)
+        relation_share()
         give_start(last, 1)
-        relation_share()
         give_start(last, 2)
-        for group in range(last):
-            add_up_all(group)
-        spread(last, 0)
+        if last > 0:
+            add_up_all(0)
         double_copy(0, across_far).wait_recv()
         pass_copy(across_far).start()
         relation_known(across_far)
-        relation_relay(far)
+        spread(last, 1)
         double_copy(1, beside_far).wait_recv()
         relation_known(beside_far)
-        spread(last, 1)
+        relation_relay(far)
         pass_copy(diagonal_far).wait_recv()
         relation_known(diagonal_far)
         relation_relay(across_far)
+        spread(last, 2)
         relation_relay(beside_far)
-        spread(last, 2)
         spread(last, 3)
         relation_relay(diagonal_far)
+        relation_end()
+        norm_start(1)
         add_up_all(last)
-        relation_end()
+        norm_start(0)
+        norm_end(1)
     else:
+        give_blocks(last)
         for index in range(far_size - 1):
             give_start(last, index)
         for group in range(groups):
 
-            @pl.loop(0, far_size)
+            @pl.loop(1 if group == 0 and last > 0 else 0, far_size)
             def _(index):
                 spread(group, index)
 
         for group in range(groups):
             add_up_all(group)
+        norm_start(0)
+        rel_squares[...] = jnp.zeros_like(rel_squares)
+    norm_end(0)
 
     for group in range(groups):
         for step in range(1, far_size):
@@ -646,8 +702,7 @@
 
 def exchange_step(inputs, sizes, collective_id):
     near_size, far_size, groups, slots, merged, group_len, width_neg, rel_count = sizes
-    table = inputs[0]
-    rows_here, columns = table.shape
+    rows_here, columns = inputs[0].shape
     parts = lax.axis_size("dim")
     dma = pltpu.SemaphoreType.DMA
     low = jnp.bfloat16
@@ -655,6 +710,8 @@
     request_count = 2 * group_len + width_neg
     in_kernel_sum = sums_in_kernel(columns, near_size, far_size)
     scratch = {
+        "table": pltpu.VMEM((rows_here, columns), low),
+        "ent_all": pltpu.VMEM((parts, 8, rows_here), jnp.float32),
         "near_out": pltpu.VMEM((groups, near_size, far_size, slots, columns), low),
         "near_in": pltpu.VMEM((groups, far_size, near_size, slots, columns), low),
         "far_out": pltpu.VMEM((groups, far_size, merged, columns), low),
@@ -671,13 +728,14 @@
     }
     for name, shape in (
         ("near", (groups, near_size, far_size)), ("far", (groups, far_size)),
-        ("part", (groups, parts)), ("give", (groups, far_size)),
+        ("part", (groups, parts)), ("give", (groups, far_size)), ("norm", (2, parts)),
         ("hand", (groups, near_size, far_size)),
     ):
         scratch[name + "_ss"] = dma(shape)
         scratch[name + "_rs"] = dma(shape)
     if in_kernel_sum:
         width = columns // near_size
+        scratch["rel_all"] = pltpu.VMEM((parts, 8, rel_count), jnp.float32)
         scratch["tiles_out"] = pltpu.VMEM((near_size, groups * group_len, width), low)
         scratch["tiles_in"] = pltpu.VMEM((near_size, groups * group_len, width), low)
         scratch["rel_part"] = pltpu.VMEM((rel_count, width), low)
@@ -693,18 +751,19 @@
     rel_rows_out = rel_count if in_kernel_sum else groups * group_len
 
     def kernel(*refs):
-        step_kernel(sizes, refs[:6], refs[6:9], dict(zip(names, refs[9:])))
+        step_kernel(sizes, refs[:7], refs[7:11], dict(zip(names, refs[11:])))
 
     return pl.pallas_call(
         kernel,
         name="exchange_step",
         out_shape=(
             jax.ShapeDtypeStruct((rows_here, columns), jnp.float32),
-            jax.ShapeDtypeStruct((rows_here, 1), jnp.float32),
+            jax.ShapeDtypeStruct((8, rows_here), jnp.float32),
             jax.ShapeDtypeStruct((rel_rows_out, columns), low),
+            jax.ShapeDtypeStruct((8, rel_count), jnp.float32),
         ),
-        in_specs=[vmem] * 6,
-        out_specs=(vmem,) * 3,
+        in_specs=[vmem] * 7,
+        out_specs=(vmem,) * 4,
         scratch_shapes=list(scratch.values()),
         compiler_params=pltpu.CompilerParams(
             collective_id=collective_id, has_side_effects=True, vmem_limit_bytes=VMEM_LIMIT
@@ -782,7 +841,6 @@
     far_size = owners // near_size
     most = min(near_size * slots, request_count)
     few = min(most, 16 * ((19 * slots + 127) // 128))
-    ent_low = entities.astype(jnp.bfloat16)
     head_ids = triples[0].reshape(groups_here, group_len)
     tail_ids = triples[2].reshape(groups_here, group_len)
     wanted = jnp.concatenate([head_ids, tail_ids, negatives], axis=1)
@@ -815,19 +873,20 @@
         sizes = (near_size, far_size, groups_here, slots, merged, group_len, width_neg, rel_count)
         return lambda *inputs: exchange_step(inputs, sizes, collective_id)
 
-    operands = (ent_low, own_ids, line_maps, place, rel_rows, plane_rel)
-    totals, counts, rel_grad = lax.cond(longest <= few, run(few, 0), run(most, 1), *operands)
+    weights = 3.0 * REG_WEIGHT * (buckets.astype(jnp.float32) + 1.0)
+    weights = jnp.broadcast_to(weights[None, :], (8, rows_here))
+    operands = (entities, own_ids, line_maps, place, rel_rows, plane_rel, weights)
+    totals, ent_all, rel_grad, rel_all = lax.cond(
+        longest <= few, run(few, 0), run(most, 1), *operands
+    )
     if rel_grad.shape[0] != rel_count:
         near, far = teams(near_size, far_size)
         near_ids = lax.all_gather(triples[1], "ent", axis_index_groups=near, tiled=True)
         rel_grad = sum_relations(rel_grad, near_ids, rel_count, near, far)
+        rel_all = lax.psum(jnp.sum(rel_grad.astype(jnp.float32) ** 2, axis=-1), "dim")[None]
     rel_grad = rel_grad.astype(jnp.float32)
-    weight = REG_WEIGHT * (buckets.astype(jnp.float32) + 1.0) * counts[:, 0]
-    totals = totals + weight[:, None] * 3.0 * entities * jnp.abs(entities)
-    ent_squares = jnp.sum(totals * totals, axis=-1)
-    ent_all, rel_all = lax.psum((ent_squares, jnp.sum(rel_grad * rel_grad, axis=-1)), "dim")
-    new_relations = adagrad(relations, rel_state, rel_grad, rel_all)
-    new_entities = adagrad(entities, ent_state, totals, ent_all)
+    new_relations = adagrad(relations, rel_state, rel_grad, rel_all[0])
+    new_entities = adagrad(entities, ent_state, totals, ent_all[0])
     return (new_entities, new_relations)
 
 

time: 261 us -> 254 us (0.973)
  the two profiles are of different devices: /device:TPU:13 before, /device:TPU:25 now
where the time goes in v4:
time: 254 us
  Pallas kernels  222 us (87%)
  other arithmetic  18.7 us (7%)
  local copies, waits for them, and re-layouts  9.44 us (4%)
  between operations  2.81 us (1%)
    pallas_call x1, Pallas kernels, exchange_step(): pl.pallas_call(kernel, name='exchange_step', out_shape=(jax.ShapeDtypeStr...  213 us
    sub x2, other arithmetic, adagrad(): return table - grad * scale[:, None]  12.2 us
    pallas_call x1, Pallas kernels, share_ids(): pl.pallas_call(functools.partial(ids_kernel, sizes), name='share_ids', ou...  9.25 us
    gather x1, local copies, waits for them, and re-layouts, per_device(): jnp.take(relations, triples[1], axis=0, mode='clip').astype(jnp.bfloat16)  5.36 us

profile of v4, /device:TPU:25, one launch (start us, length us, event | category | flops | bytes accessed | tf_op | source)
XLA Modules:
  0.0 254.1 jit_solution(12213844274233483530)
XLA Ops:
  0.7 0.8 slice_reduce_fusion.1
  1.5 0.7 constant_dynamic-update-slice_fusion
  2.2 0.7 convert_element_type.93
  2.9 0.1 and_select_fusion.2
  3.0 0.6 broadcast_in_dim.90.rel_ids
  3.6 0.3 fusion.2
  3.9 0.4 select_reduce_fusion.4
  4.4 0.6 convert_reduce_fusion
  5.0 0.6 convert_reduce_fusion.1
  7.0 1.5 select_reduce_fusion.1
  8.5 1.5 select_reduce_fusion
  10.1 0.7 pad_select_fusion.ids
  10.8 0.6 pad.13.maps
  11.4 9.2 %share_ids.1 = (s32[4,4,8,128]{3,2,1,0:T(8,128)S(1)}, s32[4,8,512]{2,1,0:T(8,128)S(1)}, s32[4,8,512]{2,1,0:T(8,128)S(1)}) custom-call(s32[4,4,8,128]{3,2,1,0:T(8,128)} %pad_select_fusion.ids, s32[4,8,512]{2,1,0:T(8,128)} %pad.13.maps, s32[8,512]{1,0:T(8,128)} %broadcast_in_dim.90.rel_ids), custom_call_target="tpu_custom_call" | custom-call | tf_op jit(solution)/shard_map/share_ids/pallas_call | solution.py:158
  20.7 0.6 slice_reduce_fusion
  22.0 5.4 %gather_fusion = bf16[512,512]{1,0:T(8,128)(2,1)S(1)} fusion(f32[4096,512]{1,0:T(8,128)} %param.12, s32[1024]{0:T(1024)S(1)} %pad_clamp_fusion), kind=kCustom, calls=%fused_computation | custom fusion | bytes 1050624 | tf_op jit(solution)/shard_map/jit(_take)/gather | solution.py:863
  27.3 0.0 copy-start.1
  27.4 0.0 copy-start.2
  27.4 214.5 %conditional.1 = ((f32[2048,512]{1,0:T(8,128)}, f32[8,2048]{1,0:T(8,128)S(1)}, bf16[4096,512]{1,0:T(8,128)(2,1)}, f32[8,4096]{1,0:T(8,128)S(1)})) conditional(s32[]{:T(128)} %convert_element_type.89, (f32[2048,512]{1,0:T(8,128)}, s32[4,4,8,128]{3,2,1,0:T(8,128)S(1)}, s32[4,8,512]{2,1,0:T(8,128)S(1)}, s32[4,768]{1,0:T(4,128)S(1)}, ...), branch_computations={%region_11.12_spmd.clone, %region_12.13_spmd.clone} | conditional | flops 4096 | bytes 126988 | solution.py:879
  27.6 0.6 pad.18.refs_3_
  28.2 0.6 broadcast_in_dim.96.refs_6_
  28.9 213.0 %exchange_step.3 = (f32[2048,512]{1,0:T(8,128)}, f32[8,2048]{1,0:T(8,128)S(1)}, bf16[4096,512]{1,0:T(8,128)(2,1)}, f32[8,4096]{1,0:T(8,128)S(1)}) custom-call(f32[2048,512]{1,0:T(8,128)} %get-tuple-element.123.refs_0_, s32[4,4,8,128]{3,2,1,0:T(8,128)S(1)} %get-tuple-element.124.refs_1_, s32[4,8,512]{2,1,0:T(8,128)S(1)} %get-tuple-element.125.refs_2_, ...), custom_call_target="tpu_custom_call" | custom-call | tf_op jit(solution)/shard_map/cond/branch_1_fun/exchange_step/pallas_call | solution.py:756
  242.0 6.1 %multiply_subtract_fusion = f32[2048,512]{1,0:T(8,128)} fusion(f32[2048,512]{1,0:T(8,128)} %param.9, f32[2048,512]{1,0:T(8,128)} %get-tuple-element.147, f32[2048]{0:T(1024)S(1)} %rsqrt_multiply_fusion.1), kind=kLoop, calls=%fused_computation.11 | loop fusion | flops 2097152 | bytes 12591104 | tf_op jit(solution)/shard_map/sub | solution.py:829
  248.1 6.1 %fusion = f32[4096,512]{1,0:T(8,128)} fusion(f32[4096,512]{1,0:T(8,128)} %param.12, bf16[4096,512]{1,0:T(8,128)(2,1)S(1)} %copy-done, f32[4096]{0:T(1024)S(1)} %rsqrt_multiply_fusion), kind=kLoop, calls=%fused_computation.4 | loop fusion | flops 6291456 | bytes 20987904 | tf_op jit(solution)/shard_map/sub | solution.py:829
  (30 shorter events, 0.2 us)
Async XLA Ops:
  27.3 214.5 %copy-start.1 = (f32[4096]{0:T(1024)S(1)}, f32[4096]{0:T(1024)}, u32[]{:S(2)}) copy-start(f32[4096]{0:T(1024)} %param.13) | copy-start | bytes 49156
  27.4 214.6 %copy-start.2 = (f32[2048]{0:T(1024)S(1)}, f32[2048]{0:T(1024)}, u32[]{:S(2)}) copy-start(f32[2048]{0:T(1024)} %param.10) | copy-start | bytes 24580
  241.9 6.1 %copy-start = (bf16[4096,512]{1,0:T(8,128)(2,1)S(1)}, bf16[4096,512]{1,0:T(8,128)(2,1)}, u32[]{:S(2)}) copy-start(bf16[4096,512]{1,0:T(8,128)(2,1)} %get-tuple-element.145) | copy-start | bytes 12582916

commit v5 on v4

--- a/solution.py
+++ b/solution.py
@@ -93,7 +93,7 @@
     return former * parts[0] - swapped(former) * parts[1]
 
 
-def ids_kernel(sizes, ids, maps, rel_ids, own_ids, line_maps, plane_rel, line_ids, *sems):
+def ids_kernel(sizes, ids, maps, rel_ids, own_ids, line_maps, plane_rel, line_ids, ids_out, *sems):
     near_size, far_size = sizes
     ids_ss, ids_rs, maps_ss, maps_rs, fwd_ss, fwd_rs, rid_ss, rid_rs = sems
     far, near = position(near_size)
@@ -109,7 +109,7 @@
 
     def ids_copy(step):
         there, peer = line_peer(step)
-        return send(ids.at[there], line_ids.at[far], ids_ss.at[step], ids_rs.at[step], peer)
+        return send(ids_out.at[there], line_ids.at[far], ids_ss.at[step], ids_rs.at[step], peer)
 
     def maps_copy(step):
         there, peer = line_peer(step)
@@ -123,6 +123,15 @@
         there, peer = near_peer(step)
         return send(rel_ids, plane_rel.at[near], rid_ss.at[step], rid_rs.at[step], peer)
 
+    longest = jnp.full((8, 128), -1, jnp.int32)
+    for there in range(far_size):
+        for first in range(0, maps.shape[2], 128):
+            longest = jnp.maximum(longest, maps[there, :, first : first + 128])
+    longest = jnp.max(longest + 1, axis=0, keepdims=True)
+    is_last = lax.broadcasted_iota(jnp.int32, (8, 128), 0) == 7
+    for there in range(far_size):
+        for beside in range(near_size):
+            ids_out[there, beside] = jnp.where(is_last, longest, ids[there, beside])
     for step in range(1, far_size):
         ids_copy(step).start()
     for step in range(1, far_size):
@@ -130,7 +139,7 @@
     for step in range(1, near_size):
         rel_ids_copy(step).start()
     plane_rel[near] = rel_ids[...]
-    line_ids[far] = ids[far]
+    line_ids[far] = ids_out[far]
     line_maps[far] = maps[far]
     for step in range(1, far_size):
         ids_copy(step).wait()
@@ -165,7 +174,7 @@
         ),
         in_specs=[vmem] * 3,
         out_specs=(vmem,) * 3,
-        scratch_shapes=[pltpu.VMEM(ids.shape, jnp.int32)]
+        scratch_shapes=[pltpu.VMEM(ids.shape, jnp.int32)] * 2
         + [dma((far_size,))] * 4
         + [dma((near_size,))] * 4,
         compiler_params=pltpu.CompilerParams(collective_id=2, has_side_effects=True),
@@ -366,7 +375,7 @@
     def hand_copy(group, step, there):
         beside, peer = near_peer(step)
         return send(
-            s["hand_out"].at[group, there, beside], s["hand_in"].at[group, near, there],
+            s["hand_out"].at[group, there, beside], s["hand_in"].at[group, there, near],
             s["hand_ss"].at[group, step, there], s["hand_rs"].at[group, step, there], peer,
         )
 
@@ -384,42 +393,43 @@
         s["hand_out"][group, there] = rows.reshape(near_size, slots, columns)
         for step in range(1, near_size):
             hand_copy(group, step, there).start()
-        s["hand_in"][group, near, there] = s["hand_out"][group, there, near]
-
-    def add_up(group, step):
-        beside = lax.rem(near + near_size - step, near_size)
-
-        @pl.when(step != 0)
-        def _():
-            @pl.loop(0, far_size)
-            def _(there):
-                hand_copy(group, step, there).wait_recv()
-
+        s["hand_in"][group, there, near] = s["hand_out"][group, there, near]
+
+    def add_up(group, index):
+        offset = jnp.where(index == 0, 0, far_size - line_step(index - 1, far_size))
+        there = lax.rem(far + offset, far_size)
+        for step in range(1, near_size):
+            hand_copy(group, step, there).wait_recv()
         if slots % 128 == 0:
             targets = jnp.concatenate(
-                [own_ids[beside, there][group : group + 1, :slots] for there in range(far_size)], axis=1
+                [own_ids[beside, there][group : group + 1, :slots] for beside in range(near_size)], axis=1
             )
-            rows = s["hand_in"][group, beside].reshape(far_size * slots, columns)
+            rows = s["hand_in"][group, there].reshape(near_size * slots, columns)
             chunk = 512 if rows_here % 512 == 0 else rows_here
 
             @pl.loop(0, rows_here // chunk)
-            def _(index):
-                first = pl.multiple_of(index * chunk, chunk)
-                hits = lax.broadcasted_iota(jnp.int32, (chunk, far_size * slots), 0) == targets - first
+            def _(part):
+                first = pl.multiple_of(part * chunk, chunk)
+                hits = lax.broadcasted_iota(jnp.int32, (chunk, near_size * slots), 0) == targets - first
                 totals[pl.ds(first, chunk)] += dot(one_hot(hits), rows)
 
         else:
 
-            @pl.loop(0, far_size)
-            def _(there):
+            @pl.loop(0, near_size)
+            def _(beside):
                 targets = own_ids[beside, there][group : group + 1, :slots]
                 hits = lax.broadcasted_iota(jnp.int32, (rows_here, slots), 0) == targets
-                totals[...] += dot(one_hot(hits), s["hand_in"][group, beside, there])
+                totals[...] += dot(one_hot(hits), s["hand_in"][group, there, beside])
 
     def add_up_all(group):
-        @pl.loop(0, near_size)
-        def _(step):
-            add_up(group, step)
+        @pl.loop(0, far_size)
+        def _(index):
+            add_up(group, index)
+
+    def span_of(act, group, first, end):
+        @pl.loop(first, end)
+        def _(index):
+            act(group, index)
 
     share_len = rel_count // far_size
     beside_far = far + 1 - 2 * lax.rem(far, 2)
@@ -479,23 +489,26 @@
         block = rel_block(row, column, way)
         return send(block, block, s["relay_ss"].at[way, row], s["relay_rs"].at[way, row], plane(peer))
 
-    def relation_parts():
-        for group in range(groups):
-            for step in range(1, near_size):
-                tiles_copy(group, step).wait_recv()
+    def relation_parts(group):
+        for step in range(1, near_size):
+            tiles_copy(group, step).wait_recv()
         chunk = 512 if rel_count % 512 == 0 else rel_count
+        of_group = slice(group * group_len, (group + 1) * group_len)
 
         @pl.loop(0, rel_count // chunk)
         def _(index):
-            first = index * chunk
+            first = pl.multiple_of(index * chunk, chunk)
             total = jnp.zeros((chunk, columns // near_size), jnp.float32)
+            if group > 0:
+                total += s["rel_part"][pl.ds(first, chunk)].astype(jnp.float32)
             for beside in range(near_size):
-                at = plane_rel[beside][:1] - first
-                hits = lax.broadcasted_iota(jnp.int32, (chunk, groups * group_len), 0) == at
-                total += dot(one_hot(hits), s["tiles_in"][beside])
-            s["rel_part"][pl.ds(pl.multiple_of(first, chunk), chunk)] = total.astype(jnp.bfloat16)
-
-        for index in range(2):
+                at = plane_rel[beside][:1, of_group] - first
+                hits = lax.broadcasted_iota(jnp.int32, (chunk, group_len), 0) == at
+                total += dot(one_hot(hits), s["tiles_in"][beside, of_group])
+            s["rel_part"][pl.ds(first, chunk)] = total.astype(jnp.bfloat16)
+
+    def relation_halve():
+        for index in (1, 0):
             halve_copy(index).start()
 
     def part_rows(row):
@@ -612,43 +625,47 @@
         give_blocks(group)
         for index in range(far_size - 1):
             give_start(group, index)
+        if in_kernel_sum:
+            relation_parts(group)
 
     if last > 0:
         spread(0, 0)
     compute(last)
     if in_kernel_sum:
-        for index in range(1, far_size - 1):
-            if last > 0:
-                spread(0, index)
-        relation_parts()
+        if last > 0:
+            spread(0, 1)
         give_blocks(last)
+        relation_parts(last)
+        relation_halve()
         give_start(last, 0)
         if last > 0:
-            spread(0, far_size - 1)
+            span_of(spread, 0, 2, 4)
         relation_across()
-        spread(last, 0)
+        span_of(spread, last, 0, 2)
         relation_share()
         give_start(last, 1)
         give_start(last, 2)
-        if last > 0:
-            add_up_all(0)
+        double_copy(1, beside_far).wait_recv()
+        relation_known(beside_far)
         double_copy(0, across_far).wait_recv()
         pass_copy(across_far).start()
         relation_known(across_far)
-        spread(last, 1)
-        double_copy(1, beside_far).wait_recv()
-        relation_known(beside_far)
         relation_relay(far)
         pass_copy(diagonal_far).wait_recv()
         relation_known(diagonal_far)
+        relation_relay(beside_far)
+        spread(last, 2)
         relation_relay(across_far)
-        spread(last, 2)
-        relation_relay(beside_far)
+        if last > 0:
+            span_of(add_up, 0, 0, 2)
         spread(last, 3)
         relation_relay(diagonal_far)
+        if last > 0:
+            span_of(add_up, 0, 2, 4)
+        span_of(add_up, last, 0, 2)
         relation_end()
         norm_start(1)
-        add_up_all(last)
+        span_of(add_up, last, 2, 4)
         norm_start(0)
         norm_end(1)
     else:
@@ -724,7 +741,7 @@
         "give_out": pltpu.VMEM((groups, far_size, merged, columns), low),
         "give_in": pltpu.VMEM((groups, far_size, merged, columns), low),
         "hand_out": pltpu.VMEM((groups, far_size, near_size, slots, columns), low),
-        "hand_in": pltpu.VMEM((groups, near_size, far_size, slots, columns), low),
+        "hand_in": pltpu.VMEM((groups, far_size, near_size, slots, columns), low),
     }
     for name, shape in (
         ("near", (groups, near_size, far_size)), ("far", (groups, far_size)),
@@ -855,8 +872,6 @@
     slot_ids = jnp.pad(
         slot_ids, ((0, 0), (0, 0), (0, 8 - groups_here), (0, 128 - slots)), constant_values=-1
     )
-    is_last_row = jnp.arange(8, dtype=jnp.int32)[:, None] == 7
-    slot_ids = jnp.where(is_last_row, jnp.max(plane_rank) + 1, slot_ids)
     slot_maps = jnp.stack([each[3] for each in placed])
     slot_maps = slot_maps.reshape(groups_here, far_size, near_size * slots).transpose(1, 0, 2)
     slot_maps = jnp.pad(slot_maps, ((0, 0), (0, 8 - groups_here), (0, 0)), constant_values=-1)
@@ -864,7 +879,7 @@
     rel_ids = jnp.broadcast_to(triples[1][None, :], (8, triples.shape[1]))
 
     own_ids, line_maps, plane_rel = share_ids(slot_ids, slot_maps, rel_ids, (near_size, far_size))
-    longest = jnp.max(own_ids[:, 0, 7, 0])
+    longest = jnp.max(own_ids[:, 0, 7])
     place = jnp.pad(
         jnp.concatenate([plane_of, plane_rank]), ((0, 8 - 2 * groups_here), (0, 0)), constant_values=-1
     )

time: 254 us -> 238 us (0.937)
  the two profiles are of different devices: /device:TPU:25 before, /device:TPU:13 now
where the time goes in v5:
time: 238 us; the launch traced here: 234 us
  Pallas kernels  205 us (86%)
  other arithmetic  16.8 us (7%)
  local copies, waits for them, and re-layouts  10.1 us (4%)
    pallas_call x1, Pallas kernels, exchange_step(): pl.pallas_call(kernel, name='exchange_step', out_shape=(jax.ShapeDtypeStr...  196 us
    sub x2, other arithmetic, adagrad(): return table - grad * scale[:, None]  12.2 us
    pallas_call x1, Pallas kernels, share_ids(): pl.pallas_call(functools.partial(ids_kernel, sizes), name='share_ids', ou...  8.64 us
    gather x1, local copies, waits for them, and re-layouts, per_device(): jnp.take(relations, triples[1], axis=0, mode='clip').astype(jnp.bfloat16)  5.36 us

profile of v5, /device:TPU:13, one launch (start us, length us, event | category | flops | bytes accessed | tf_op | source)
XLA Modules:
  0.0 233.9 jit_solution(14607911729801075889)
XLA Ops:
  0.6 0.8 slice_reduce_fusion.1
  1.5 0.7 constant_dynamic-update-slice_fusion
  2.2 0.7 convert_element_type.91
  2.9 0.1 and_select_fusion.2
  3.0 0.6 broadcast_in_dim.75.rel_ids
  3.6 0.3 fusion.1
  3.9 0.4 select_reduce_fusion.5
  4.4 1.5 select_reduce_fusion.1
  5.9 1.5 select_reduce_fusion
  7.5 0.6 pad.12.ids
  8.2 0.6 pad.13.maps
  8.8 8.6 %share_ids.1 = (s32[4,4,8,128]{3,2,1,0:T(8,128)S(1)}, s32[4,8,512]{2,1,0:T(8,128)S(1)}, s32[4,8,512]{2,1,0:T(8,128)S(1)}) custom-call(s32[4,4,8,128]{3,2,1,0:T(8,128)} %pad.12.ids, s32[4,8,512]{2,1,0:T(8,128)} %pad.13.maps, s32[8,512]{1,0:T(8,128)} %broadcast_in_dim.75.rel_ids), custom_call_target="tpu_custom_call" | custom-call | tf_op jit(solution)/shard_map/share_ids/pallas_call | solution.py:167
  17.5 0.6 slice_reduce_fusion
  18.8 5.4 %gather_fusion = bf16[512,512]{1,0:T(8,128)(2,1)S(1)} fusion(f32[4096,512]{1,0:T(8,128)} %param.12, s32[1024]{0:T(1024)S(1)} %pad_clamp_fusion), kind=kCustom, calls=%fused_computation | custom fusion | bytes 1050624 | tf_op jit(solution)/shard_map/jit(_take)/gather | solution.py:878
  24.1 0.0 copy-start.1
  24.1 0.0 copy-start.2
  24.2 197.5 %conditional.1 = ((f32[2048,512]{1,0:T(8,128)}, f32[8,2048]{1,0:T(8,128)S(1)}, bf16[4096,512]{1,0:T(8,128)(2,1)}, f32[8,4096]{1,0:T(8,128)S(1)})) conditional(s32[]{:T(128)} %convert_element_type.87, (f32[2048,512]{1,0:T(8,128)}, s32[4,4,8,128]{3,2,1,0:T(8,128)S(1)}, s32[4,8,512]{2,1,0:T(8,128)S(1)}, s32[4,768]{1,0:T(4,128)S(1)}, ...), branch_computations={%region_9.10_spmd.clone, %region_10.11_spmd.clone} | conditional | flops 4096 | bytes 126988 | solution.py:894
  24.4 0.6 pad.18.refs_3_
  25.0 0.6 broadcast_in_dim.81.refs_6_
  25.7 196.0 %exchange_step.3 = (f32[2048,512]{1,0:T(8,128)}, f32[8,2048]{1,0:T(8,128)S(1)}, bf16[4096,512]{1,0:T(8,128)(2,1)}, f32[8,4096]{1,0:T(8,128)S(1)}) custom-call(f32[2048,512]{1,0:T(8,128)} %get-tuple-element.123.refs_0_, s32[4,4,8,128]{3,2,1,0:T(8,128)S(1)} %get-tuple-element.124.refs_1_, s32[4,8,512]{2,1,0:T(8,128)S(1)} %get-tuple-element.125.refs_2_, ...), custom_call_target="tpu_custom_call" | custom-call | tf_op jit(solution)/shard_map/cond/branch_1_fun/exchange_step/pallas_call | solution.py:773
  221.7 0.0 copy-done.2
  221.7 6.1 %multiply_subtract_fusion = f32[2048,512]{1,0:T(8,128)} fusion(f32[2048,512]{1,0:T(8,128)} %param.9, f32[2048,512]{1,0:T(8,128)} %get-tuple-element.147, f32[2048]{0:T(1024)S(1)} %rsqrt_multiply_fusion.1), kind=kLoop, calls=%fused_computation.11 | loop fusion | flops 2097152 | bytes 12591104 | tf_op jit(solution)/shard_map/sub | solution.py:846
  227.8 0.0 copy-done
  227.8 6.1 %fusion = f32[4096,512]{1,0:T(8,128)} fusion(f32[4096,512]{1,0:T(8,128)} %param.12, bf16[4096,512]{1,0:T(8,128)(2,1)S(1)} %copy-done, f32[4096]{0:T(1024)S(1)} %rsqrt_multiply_fusion), kind=kLoop, calls=%fused_computation.4 | loop fusion | flops 6291456 | bytes 20987904 | tf_op jit(solution)/shard_map/sub | solution.py:846
  (29 shorter events, 0.2 us)
Async XLA Ops:
  24.1 197.5 %copy-start.1 = (f32[4096]{0:T(1024)S(1)}, f32[4096]{0:T(1024)}, u32[]{:S(2)}) copy-start(f32[4096]{0:T(1024)} %param.13) | copy-start | bytes 49156
  24.1 197.6 %copy-start.2 = (f32[2048]{0:T(1024)S(1)}, f32[2048]{0:T(1024)}, u32[]{:S(2)}) copy-start(f32[2048]{0:T(1024)} %param.10) | copy-start | bytes 24580
  221.7 6.1 %copy-start = (bf16[4096,512]{1,0:T(8,128)(2,1)S(1)}, bf16[4096,512]{1,0:T(8,128)(2,1)}, u32[]{:S(2)}) copy-start(bf16[4096,512]{1,0:T(8,128)(2,1)} %get-tuple-element.145) | copy-start | bytes 12582916
